TPU v7x, 128 devices: a whole 4x4x4 slice. The times are simulated.
128 devices in a mesh: seq: 64 (over z, x, y), batch: 2 (over core).
Axes of the slice: x: 4, y: 4, z: 4, core: 2. Of those that a mesh axis runs over, the one named last changes fastest.
Arguments:
- inputs: bfloat16 [2, 8192, 2048], P('batch', 'seq'), may hold values from -6 to 6
- cotangent: bfloat16 [2, 8192, 1024], P('batch', 'seq'), may hold values from -48 to 48
- w_query: bfloat16 [2048, 128], replicated, may hold values from -0.125 to 0.125
- w_key: bfloat16 [2048, 128], replicated, may hold values from -0.125 to 0.125
- w_value: bfloat16 [2048, 1024], replicated, may hold values from -0.125 to 0.125
Outputs:
- grad_inputs: bfloat16 [2, 8192, 2048], P('batch', 'seq')
- grad_w_query: float32 [2048, 128], P(('seq', 'batch'))
- grad_w_key: float32 [2048, 128], P(('seq', 'batch'))
- grad_w_value: float32 [2048, 1024], P(('seq', 'batch'))
All inputs are finite; a program needn't handle non-finite values.
Results may differ from a plain program's by a relative error of at most 0.006.
Values sent between devices are 32-bit elements; how exact they have to be, the bound alone decides.
A program may use at most 128 MiB of HBM per device.

v0:
```python
import math

import jax
import jax.numpy as jnp
import numpy as np
from jax import lax
from jax.sharding import Mesh
from jax.sharding import PartitionSpec as P

D = 2048
H = 8
DK = 16
DV = 128
SEQ = ("seq_0", "seq_1", "seq_2")
SEQ_BATCH = ("seq_0", "seq_1", "seq_2", "batch")


highest = lax.Precision.HIGHEST
threepass = lax.Precision.HIGH


def nothing_yet(shard, identity):
    return jax.tree.map(
        lambda part, zero: jnp.zeros_like(part) + jnp.asarray(zero, part.dtype), shard, identity
    )


def entering(shard, axes, combine, identity, reverse):
    before = start = nothing_yet(shard, identity)
    total = shard
    for axis in reversed(axes):
        size, place = (lax.axis_size(axis), lax.axis_index(axis))
        pieces = jax.tree.map(lambda part: lax.all_gather(part, axis), total)
        inside, total = (start, start)
        for k in reversed(range(size)) if reverse else range(size):
            passed = k > place if reverse else k < place
            total = combine(total, jax.tree.map(lambda part: part[k], pieces))
            inside = jax.tree.map(lambda new, old: jnp.where(passed, new, old), total, inside)
        before = combine(inside, before)
    return before


def in_blocks(shard, dim, size):
    dims = shard.shape
    pieces = shard.reshape(*dims[:dim], size, dims[dim] // size, *dims[dim + 1 :])
    return jnp.moveaxis(pieces, dim, 0)


def summed_on_arrival(shard, axis, dim):
    pieces = in_blocks(shard, dim, lax.axis_size(axis))
    arrived = lax.all_to_all(pieces, axis, split_axis=0, concat_axis=0, tiled=True)
    return arrived.sum(axis=0)


def scatter_axes(shard, axes, dim):
    for axis in axes:
        shard = lax.psum_scatter(shard, axis, scatter_dimension=dim, tiled=True)
    return shard


def pair_tables(width):
    rows_idx, cols_idx = np.triu_indices(width)
    eye_table = np.eye(width, dtype=np.float32)
    left_pick = jnp.asarray(eye_table[rows_idx])
    right_pick = jnp.asarray(eye_table[cols_idx])
    pair_coef = jnp.asarray(
        np.where(rows_idx == cols_idx, 1.0 / math.sqrt(2.0), 1.0).astype(np.float32)
    )
    return (left_pick, right_pick, pair_coef)


def features(scaled, tables):
    left_pick, right_pick, pair_coef = tables
    left_val = jnp.einsum("...d,pd->...p", scaled, left_pick, precision=highest)
    right_val = jnp.einsum("...d,pd->...p", scaled, right_pick, precision=highest)
    leading = jnp.ones(scaled.shape[:-1] + (1,), jnp.float32)
    return jnp.concatenate([leading, scaled, left_val * right_val * pair_coef], -1)


def pull_back(scaled, grad_feat, tables):
    left_pick, right_pick, pair_coef = tables
    width = scaled.shape[-1]
    linear_part = grad_feat[..., 1 : 1 + width]
    pair_grad = grad_feat[..., 1 + width :] * pair_coef
    left_val = jnp.einsum("...d,pd->...p", scaled, left_pick, precision=highest)
    right_val = jnp.einsum("...d,pd->...p", scaled, right_pick, precision=highest)
    result = linear_part + jnp.einsum(
        "...p,pd->...d", pair_grad * right_val, left_pick, precision=highest
    )
    return result + jnp.einsum("...p,pd->...d", pair_grad * left_val, right_pick, precision=highest)


def add_pair(earlier, later):
    return (earlier[0] + later[0], earlier[1] + later[1])


def times_transposed(left, right):
    return lax.dot_general(
        left, right, (((1,), (1,)), ((), ())), preferred_element_type=jnp.float32
    )


def body(inputs, cotangent, w_query, w_key, w_value):
    tables = pair_tables(DK)
    tokens = inputs[0]
    length = tokens.shape[0]
    query = jnp.dot(tokens, w_query, preferred_element_type=jnp.float32).reshape(length, H, DK)
    keys = jnp.dot(tokens, w_key, preferred_element_type=jnp.float32).reshape(length, H, DK)
    values = (
        jnp.dot(tokens, w_value, preferred_element_type=jnp.float32)
        .astype(jnp.bfloat16)
        .reshape(length, H, DV)
    )
    feat_q = features(query * 0.5, tables).astype(jnp.bfloat16)
    feat_k = features(keys * 0.5, tables).astype(jnp.bfloat16)
    upstream = cotangent[0].astype(jnp.float32).reshape(length, H, DV)
    fq32 = feat_q.astype(jnp.float32)
    fk32 = feat_k.astype(jnp.float32)
    val32 = values.astype(jnp.float32)
    causal = lax.broadcasted_iota(jnp.int32, (length, length), 0) >= lax.broadcasted_iota(
        jnp.int32, (length, length), 1
    )
    attn = jnp.einsum("thf,shf->hts", feat_q, feat_k, preferred_element_type=jnp.float32)
    attn = jnp.where(causal, attn, 0.0)
    local_state = jnp.einsum("shf,she->hfe", feat_k, values, preferred_element_type=jnp.float32)
    local_norm = jnp.sum(fk32, 0)
    zero_pair = (jnp.zeros_like(local_state), jnp.zeros_like(local_norm))
    state, norm_state = entering((local_state, local_norm), SEQ, add_pair, zero_pair, False)
    numerator = jnp.einsum("hts,she->the", attn, val32, precision=threepass)
    numerator = numerator + jnp.einsum("thf,hfe->the", fq32, state, precision=threepass)
    denominator = jnp.transpose(jnp.sum(attn, -1), (1, 0))
    denominator = denominator + jnp.einsum("thf,hf->th", fq32, norm_state, precision=highest)
    output = numerator / denominator[..., None]
    grad_numer = upstream / denominator[..., None]
    grad_denom = -jnp.sum(upstream * output, -1) / denominator
    grad_attn = jnp.einsum("the,she->hts", grad_numer, val32, precision=threepass)
    grad_attn = jnp.where(causal, grad_attn + jnp.transpose(grad_denom, (1, 0))[:, :, None], 0.0)
    grad_fq = jnp.einsum("hts,shf->thf", grad_attn, fk32, precision=threepass)
    grad_fq = grad_fq + jnp.einsum("hfe,the->thf", state, grad_numer, precision=threepass)
    grad_fq = grad_fq + norm_state[None, :, :] * grad_denom[..., None]
    local_back = jnp.einsum("thf,the->hfe", fq32, grad_numer, precision=threepass)
    local_back_norm = jnp.einsum("thf,th->hf", fq32, grad_denom, precision=highest)
    back_state, back_norm = entering((local_back, local_back_norm), SEQ, add_pair, zero_pair, True)
    grad_val = jnp.einsum("hts,the->she", attn, grad_numer, precision=threepass)
    grad_val = grad_val + jnp.einsum("shf,hfe->she", fk32, back_state, precision=threepass)
    grad_fk = jnp.einsum("hts,thf->shf", grad_attn, fq32, precision=threepass)
    grad_fk = grad_fk + jnp.einsum("she,hfe->shf", val32, back_state, precision=threepass)
    grad_fk = grad_fk + back_norm[None, :, :]
    grad_query = (
        (pull_back(query * 0.5, grad_fq, tables) * 0.5).astype(jnp.bfloat16).reshape(length, H * DK)
    )
    grad_keys = (
        (pull_back(keys * 0.5, grad_fk, tables) * 0.5).astype(jnp.bfloat16).reshape(length, H * DK)
    )
    grad_values = grad_val.astype(jnp.bfloat16).reshape(length, H * DV)
    grad_in = (
        times_transposed(grad_query, w_query)
        + times_transposed(grad_keys, w_key)
        + times_transposed(grad_values, w_value)
    )
    grad_in = grad_in.astype(jnp.bfloat16)[None]
    joined_grads = jnp.concatenate([grad_query, grad_keys, grad_values], 1)
    n_seq = lax.axis_size(SEQ)
    n_batch = lax.axis_size("batch")
    share = D // (n_seq * n_batch)
    partial_sum = lax.dot_general(
        tokens, joined_grads, (((0,), (0,)), ((), ())), preferred_element_type=jnp.float32
    ).reshape(n_seq, n_batch, share, joined_grads.shape[1])
    partial_sum = summed_on_arrival(partial_sum, "batch", 1)
    reduced = scatter_axes(partial_sum, SEQ, 0).reshape(share, joined_grads.shape[1])
    grad_wq = reduced[:, : H * DK]
    grad_wk = reduced[:, H * DK : 2 * H * DK]
    grad_wv = reduced[:, 2 * H * DK :]
    return (grad_in, grad_wq, grad_wk, grad_wv)


def solution(mesh):
    split = Mesh(
        mesh.devices.reshape(4, 4, 4, mesh.shape["batch"]), ("seq_0", "seq_1", "seq_2", "batch")
    )
    in_specs = (P("batch", SEQ, None), P("batch", SEQ, None), P(), P(), P())
    out_specs = (P("batch", SEQ, None), P(SEQ_BATCH, None), P(SEQ_BATCH, None), P(SEQ_BATCH, None))
    return jax.shard_map(body, mesh=split, in_specs=in_specs, out_specs=out_specs, check_vma=False)
```

profile of v0, /device:TPU:0, one launch (start us, length us, event | category | flops | bytes accessed | tf_op | source)
XLA Modules:
  0.0 415.0 jit_solution(15224355229776971556)
XLA Ops:
  11.4 3.1 fusion.12
  18.4 12.6 %all-gather = f32[32,153]{1,0:T(8,128)S(1)} all-gather(f32[8,153]{1,0:T(8,128)S(1)} %convert_reduce_fusion), channel_id=2, replica_groups=mesh['seq_0'=4,'seq_1'=4,'seq_2'=4,'batch'=2] {'seq_2'}, dimensions={0}, use_global_device_ids=true | all-gather | bytes 24480 | tf_op jit(solution)/shard_map/all_gather | solution.py:33
  31.0 12.3 %all_gather.58 = f32[4,8,153]{2,1,0:T(8,128)S(1)} all-gather(f32[1,8,153]{2,1,0:T(8,128)S(1)} %fusion.64), channel_id=1, replica_groups=mesh['seq_0'=4,'seq_1'=4,'seq_2'=4,'batch'=2] {'seq_1'}, dimensions={0}, use_global_device_ids=true | all-gather | bytes 24480 | tf_op jit(solution)/shard_map/all_gather | solution.py:33
  43.2 13.1 %all_gather.59 = f32[4,8,153]{2,1,0:T(8,128)S(1)} all-gather(f32[1,8,153]{2,1,0:T(8,128)S(1)} %slice_add_fusion.30), channel_id=1, replica_groups=mesh['seq_0'=4,'seq_1'=4,'seq_2'=4,'batch'=2] {'seq_0'}, dimensions={0}, use_global_device_ids=true | all-gather | bytes 24480 | tf_op jit(solution)/shard_map/all_gather | solution.py:33
  60.0 2.6 fusion.28
  62.7 35.0 %all-gather.21.cloned.1.call-done = f32[32,153,128]{2,0,1:T(8,128)} async-done(((f32[8,153,128]{2,0,1:T(8,128)}), f32[32,153,128]{2,0,1:T(8,128)}) %all-gather.21.cloned.1.call-update) | async-done | bytes 2506768 | tf_op jit(solution)/shard_map/all_gather | solution.py:33
  100.4 34.1 %all-gather.11.cloned.1.call-done = f32[4,8,153,128]{3,1,2,0:T(8,128)} async-done(((f32[1,8,153,128]{3,1,2,0:T(8,128)}), f32[4,8,153,128]{3,1,2,0:T(8,128)}) %all-gather.11.cloned.1.call-update) | async-done | bytes 2506768 | tf_op jit(solution)/shard_map/all_gather | solution.py:33
  137.1 33.1 %all-gather.15.cloned.1.call-done = f32[4,8,153,128]{3,1,2,0:T(8,128)} async-done(((f32[1,8,153,128]{3,1,2,0:T(8,128)}), f32[4,8,153,128]{3,1,2,0:T(8,128)}) %all-gather.15.cloned.1.call-update) | async-done | bytes 2506768 | tf_op jit(solution)/shard_map/all_gather | solution.py:33
  175.4 2.7 fusion.70
  178.0 28.3 %all-gather.13.cloned.1.call-done = f32[4,8,153,128]{3,1,2,0:T(8,128)} async-done(((f32[1,8,153,128]{3,1,2,0:T(8,128)}), f32[4,8,153,128]{3,1,2,0:T(8,128)}) %all-gather.13.cloned.1.call-update) | async-done | bytes 2506768 | tf_op jit(solution)/shard_map/all_gather | solution.py:33
  206.3 3.0 fusion.27
  210.8 12.2 %all-gather.3 = f32[32,153]{1,0:T(8,128)S(1)} all-gather(f32[8,153]{1,0:T(8,128)S(1)} %bitcast.184), channel_id=5, replica_groups=mesh['seq_0'=4,'seq_1'=4,'seq_2'=4,'batch'=2] {'seq_2'}, dimensions={0}, use_global_device_ids=true | all-gather | bytes 24480 | tf_op jit(solution)/shard_map/all_gather | solution.py:33
  223.0 12.2 %all_gather.70 = f32[4,8,153]{2,1,0:T(8,128)S(1)} all-gather(f32[1,8,153]{2,1,0:T(8,128)S(1)} %fusion.61), channel_id=1, replica_groups=mesh['seq_0'=4,'seq_1'=4,'seq_2'=4,'batch'=2] {'seq_1'}, dimensions={0}, use_global_device_ids=true | all-gather | bytes 24480 | tf_op jit(solution)/shard_map/all_gather | solution.py:33
  235.3 12.3 %all_gather.71 = f32[4,8,153]{2,1,0:T(8,128)S(1)} all-gather(f32[1,8,153]{2,1,0:T(8,128)S(1)} %slice_add_fusion.21), channel_id=1, replica_groups=mesh['seq_0'=4,'seq_1'=4,'seq_2'=4,'batch'=2] {'seq_0'}, dimensions={0}, use_global_device_ids=true | all-gather | bytes 24480 | tf_op jit(solution)/shard_map/all_gather | solution.py:33
  251.4 3.0 fusion.23
  258.5 5.5 %convolution_bitcast_fusion = f32[2048,1280]{0,1:T(8,128)} fusion(bf16[1,128,2048]{2,1,0:T(8,128)(2,1)S(1)} %copy-done, bf16[128,1024]{0,1:T(8,128)(2,1)S(1)} %bitcast.163, bf16[128,128]{0,1:T(8,128)(2,1)S(1)} %bitcast.172, bf16[128,128]{0,1:T(8,128)(2,1)S(1)} %bitcast.170), kind=kOutput, calls=%fused_computation | convolution fusion | flops 672071680 | bytes 11337728 | tf_op jit(solution)/shard_map/dot_general | solution.py:166
  264.0 11.2 %copy.64 = f32[2048,1280]{1,0:T(8,128)} copy(f32[2048,1280]{0,1:T(8,128)} %convolution_bitcast_fusion) | data formatting | bytes 20971520 | tf_op jit(solution)/shard_map/dot_general | solution.py:166
  275.3 4.8 %copy.65 = f32[2,64,1,16,1280]{4,3,1,2,0:T(8,128)S(1)} copy(f32[2,64,1,16,1280]{4,3,0,1,2:T(8,128)} %bitcast.159) | data formatting | bytes 20971520 | tf_op jit(solution)/shard_map/transpose | solution.py:46
  280.1 13.6 %all_to_all.5 = f32[2,64,1,16,1280]{4,3,1,2,0:T(8,128)} all-to-all(f32[2,64,1,16,1280]{4,3,1,2,0:T(8,128)S(1)} %copy.65), channel_id=1, replica_groups=mesh['seq_0'=4,'seq_1'=4,'seq_2'=4,'batch'=2] {'batch'}, dimensions={0} | all-to-all | bytes 20971520 | tf_op jit(solution)/shard_map/all_to_all | solution.py:51
  293.8 7.8 %reduce_sum.41 = f32[64,16,1280]{2,1,0:T(8,128)} reduce(f32[2,64,1,16,1280]{4,3,1,2,0:T(8,128)} %all_to_all.5, f32[]{:T(128)} %constant.15.clone.1), dimensions={0,2}, to_apply=%region_3.4 | reduce | flops 1310720 | bytes 15728644 | tf_op jit(solution)/shard_map/reduce_sum | solution.py:52
  301.6 54.1 %reduce-scatter.4.cloned.1.call-done = f32[16,1,16,1280]{3,2,1,0:T(8,128)} async-done(((f32[64,1,16,1280]{3,2,1,0:T(8,128)}), f32[16,1,16,1280]{3,2,1,0:T(8,128)}) %reduce-scatter.4.cloned.1.call-update) | async-done | bytes 1310736 | tf_op jit(solution)/shard_map/reduce_scatter | solution.py:57
  356.1 26.2 %reduce-scatter.6.cloned.1.call-done = f32[4,1,16,1280]{3,2,1,0:T(8,128)} async-done(((f32[16,1,16,1280]{3,2,1,0:T(8,128)}), f32[4,1,16,1280]{3,2,1,0:T(8,128)}) %reduce-scatter.6.cloned.1.call-update) | async-done | bytes 327696 | tf_op jit(solution)/shard_map/reduce_scatter | solution.py:57
  382.7 4.5 %fusion.1 = bf16[1,128,2048]{2,1,0:T(8,128)(2,1)} fusion(f32[128,2048]{1,0:T(8,128)S(1)} %convolution_add_fusion.1, bf16[128,1024]{0,1:T(8,128)(2,1)S(1)} %bitcast.164, bf16[2048,1024]{1,0:T(8,128)(2,1)} %param.12), kind=kOutput, calls=%fused_computation.4 | convolution fusion | flops 537395200 | bytes 6029312 | tf_op jit(solution)/shard_map/dot_general | solution.py:98
  387.2 18.4 %reduce-scatter.8.cloned.1.call-done = f32[1,1,16,1280]{3,2,1,0:T(8,128)} async-done(((f32[4,1,16,1280]{3,2,1,0:T(8,128)}), f32[1,1,16,1280]{3,2,1,0:T(8,128)}) %reduce-scatter.8.cloned.1.call-update) | async-done | bytes 81936 | tf_op jit(solution)/shard_map/reduce_scatter | solution.py:57
  (131 shorter events, 34.8 us)
Async XLA Ops:
  7.2 3.0 copy-start.19
  7.2 52.8 %all-gather.19.cloned.1.call-start = ((), (), s32[]{:S(2)}) async-start(), calls=%async_computation.11 | async-start | bytes 3133440 | tf_op jit(solution)/shard_map/all_gather | solution.py:33
  9.6 5.0 %copy-start.6 = (f32[128,8,136]{0,2,1:T(8,128)}, f32[128,8,136]{0,2,1:T(8,128)S(1)}, u32[]{:S(2)}) copy-start(f32[128,8,136]{0,2,1:T(8,128)S(1)} %fusion.76) | copy-start | bytes 1671172
  10.2 4.4 %copy-start.8 = (f32[128,8,136]{0,2,1:T(8,128)}, f32[128,8,136]{0,2,1:T(8,128)S(1)}, u32[]{:S(2)}) copy-start(f32[128,8,136]{0,2,1:T(8,128)S(1)} %fusion.77) | copy-start | bytes 1671172
  11.4 4.7 %copy-start.4 = (f32[128,8,136]{0,2,1:T(8,128)}, f32[128,8,136]{0,2,1:T(8,128)S(1)}, u32[]{:S(2)}) copy-start(f32[128,8,136]{0,2,1:T(8,128)S(1)} %fusion.78) | copy-start | bytes 1671172
  11.4 3.2 copy-start.30
  14.6 3.1 copy-start.10
  17.7 80.0 %all-gather.21.cloned.1.call-start = ((), (), s32[]{:S(2)}) async-start(), calls=%async_computation.12 | async-start | bytes 3133440 | tf_op jit(solution)/shard_map/all_gather | solution.py:33
  17.9 40.8 %copy-start.23 = (f32[1,128,1024]{1,2,0:T(8,128)}, f32[1,128,1024]{1,2,0:T(8,128)S(1)}, u32[]{:S(2)}) copy-start(f32[1,128,1024]{1,2,0:T(8,128)S(1)} %copy.44) | copy-start | bytes 1572868
  60.0 74.5 %all-gather.11.cloned.1.call-start = ((), (), s32[]{:S(2)}) async-start(), calls=%async_computation.4 | async-start | bytes 3133440 | tf_op jit(solution)/shard_map/all_gather | solution.py:33
  62.7 107.6 %all-gather.15.cloned.1.call-start = ((), (), s32[]{:S(2)}) async-start(), calls=%async_computation.6 | async-start | bytes 3133440 | tf_op jit(solution)/shard_map/all_gather | solution.py:33
  100.3 106.0 %all-gather.13.cloned.1.call-start = ((), (), s32[]{:S(2)}) async-start(), calls=%async_computation.5 | async-start | bytes 3133440 | tf_op jit(solution)/shard_map/all_gather | solution.py:33
  137.1 114.4 %all-gather.17.cloned.1.call-start = ((), (), s32[]{:S(2)}) async-start(), calls=%async_computation.7 | async-start | bytes 3133440 | tf_op jit(solution)/shard_map/all_gather | solution.py:33
  172.8 33.5 %copy-start.2 = (f32[32,153,128]{2,0,1:T(8,128)S(1)}, f32[32,153,128]{2,0,1:T(8,128)}, u32[]{:S(2)}) copy-start(f32[32,153,128]{2,0,1:T(8,128)} %all-gather.19.cloned.1.call-done) | copy-start | bytes 7520260
  172.8 182.9 %reduce-scatter.4.cloned.1.call-start = ((), (), s32[]{:S(2)}) async-start(), calls=%async_computation.8 | async-start | bytes 6553600 | tf_op jit(solution)/shard_map/reduce_scatter | solution.py:57
  209.3 38.3 %copy-start.11 = (bf16[16,8,8,128]{3,2,1,0:T(8,128)(2,1)S(1)}, bf16[16,8,8,128]{3,2,1,0:T(8,128)(2,1)}, u32[]{:S(2)}) copy-start(bf16[16,8,8,128]{3,2,1,0:T(8,128)(2,1)} %copy-done.10) | copy-start | bytes 786436
  247.6 3.8 copy-start.3
  251.4 3.9 copy-start.12
  251.4 3.9 copy-start.15
  301.5 54.3 %copy-start.20 = (bf16[2048,128]{1,0:T(8,128)(2,1)S(1)}, bf16[2048,128]{1,0:T(8,128)(2,1)}, u32[]{:S(2)}) copy-start(bf16[2048,128]{1,0:T(8,128)(2,1)} %param.10) | copy-start | bytes 1572868
  301.6 80.8 %copy-start.21 = (bf16[2048,128]{1,0:T(8,128)(2,1)S(1)}, bf16[2048,128]{1,0:T(8,128)(2,1)}, u32[]{:S(2)}) copy-start(bf16[2048,128]{1,0:T(8,128)(2,1)} %param.11) | copy-start | bytes 1572868
  301.6 80.8 %reduce-scatter.6.cloned.1.call-start = ((), (), s32[]{:S(2)}) async-start(), calls=%async_computation.9 | async-start | bytes 1638400 | tf_op jit(solution)/shard_map/reduce_scatter | solution.py:57
  355.7 49.9 %reduce-scatter.8.cloned.1.call-start = ((), (), s32[]{:S(2)}) async-start(), calls=%async_computation.10 | async-start | bytes 409600 | tf_op jit(solution)/shard_map/reduce_scatter | solution.py:57
  382.4 26.1 %copy-start.1 = (bf16[1,128,2048]{2,1,0:T(8,128)(2,1)S(1)}, bf16[1,128,2048]{2,1,0:T(8,128)(2,1)}, u32[]{:S(2)}) copy-start(bf16[1,128,2048]{2,1,0:T(8,128)(2,1)} %param.8) | copy-start | bytes 1572868
  (16 other events, 31.4 us)
Sparse Core Ops, SparseCore 0:
  17.8 39.8 all-gather.18
  60.1 37.5 all-gather.20
  99.3 35.0 all-gather.10
  136.0 34.2 all-gather.14
  171.7 34.4 all-gather.12
  207.8 34.4 all-gather.16
  301.7 53.9 reduce-scatter.3
  358.1 24.1 reduce-scatter.5
  384.7 20.8 reduce-scatter.7
where the time goes:
time: 416 us; the launch traced here: 415 us
  waiting for transfers between devices  229 us (55%)
  blocking collectives  88.3 us (21%)
  matrix products  33.8 us (8%)
  other arithmetic  24.8 us (6%)
  local copies, waits for them, and re-layouts  23.9 us (6%)
  between operations  14.5 us (3%)
    all_gather x6, waiting for transfers between devices, entering(): pieces = jax.tree.map(lambda part: lax.all_gather(part, axis), total)  130 us
    reduce_scatter x3, waiting for transfers between devices, scatter_axes(): shard = lax.psum_scatter(shard, axis, scatter_dimension=dim, tiled=True)  98.7 us
    all_gather x6, blocking collectives, entering(): pieces = jax.tree.map(lambda part: lax.all_gather(part, axis), total)  74.7 us
    add x11, other arithmetic, add_pair(): return (earlier[0] + later[0], earlier[1] + later[1])  16.4 us
    all_to_all x1, blocking collectives, summed_on_arrival(): lax.all_to_all(pieces, axis, split_axis=0, concat_axis=0, tiled=True)  13.6 us
    dot_general x1, local copies, waits for them, and re-layouts, body(): lax.dot_general(tokens, joined_grads, (((0,), (0,)), ((), ())), preferred...  11.2 us
  transfers between devices with their start and end apart: 9, of which 7 were waited for; matrix products, arithmetic and copies ran while one was open for 8% of the time, Pallas kernels for 0%

commit v1 on v0

v1 whole, which is shorter than its diff:
```python
import math

import jax
import jax.numpy as jnp
from jax import lax
from jax.experimental import pallas as pl
from jax.experimental.pallas import tpu as pltpu
from jax.sharding import Mesh
from jax.sharding import PartitionSpec as P

D = 2048
H = 8
DK = 16
DV = 128
SEQ = ("seq_0", "seq_1", "seq_2")
SEQ_BATCH = ("seq_0", "seq_1", "seq_2", "batch")
N = 4
BLK = 128
TOK = N * BLK
FP = 160
ROOT = 1.0 / math.sqrt(2.0)
ORDER = (1, 3, 2, 0)
f32 = jnp.float32
bf16 = jnp.bfloat16
MESH_ID = pl.DeviceIdType.MESH


def mm(a, b):
    return lax.dot_general(a, b, (((1,), (0,)), ((), ())), preferred_element_type=f32)


def mm_nt(a, b):
    return lax.dot_general(a, b, (((1,), (1,)), ((), ())), preferred_element_type=f32)


def mm_tn(a, b):
    return lax.dot_general(a, b, (((0,), (0,)), ((), ())), preferred_element_type=f32)


def halves(row):
    high = row.astype(bf16).astype(f32)
    return high, row - high


def rows16(*rows):
    n = rows[0].shape[1]
    at = lax.broadcasted_iota(jnp.int32, (16, n), 0)
    out = jnp.zeros((16, n), f32)
    for i, row in enumerate(rows):
        out = jnp.where(at == i, jnp.broadcast_to(row, (16, n)), out)
    return out.astype(bf16)


def turned(u, d):
    d = d % DK
    return u if d == 0 else pltpu.roll(u, DK - d, 0)


def features(u):
    n = u.shape[1]
    parts = [u, u * u * ROOT]
    for d in range(1, 8):
        parts.append(u * turned(u, d))
    parts.append(u[:8] * u[8:])
    first = lax.broadcasted_iota(jnp.int32, (8, n), 0) == 0
    parts.append(jnp.where(first, 1.0, 0.0).astype(f32))
    return jnp.concatenate(parts, 0).astype(bf16)


def pull_back(u, g):
    out = g[0:16] + (g[16:32] * (2.0 * ROOT)) * u
    for d in range(1, 8):
        pair = g[16 + 16 * d : 32 + 16 * d]
        out = out + pair * turned(u, d) + turned(pair * u, -d)
    pair = g[144:152]
    return out + jnp.concatenate([pair * u[8:], pair * u[:8]], 0)


def kernel(
    x_hbm, u_hbm, wq_hbm, wk_hbm, wv_hbm,
    gin, gwq, gwk, gwv,
    xb, ub, wq, wk, wv, xt2, xg,
    sqk, sv, rqk, rv, us, ur,
    fq, fk, vb, vt, ut, at, num, dloc, gnb, gdr, gfq, gfk, gvt, stb, nrm,
    st1, xr1, zs1, zr1, pb1, pf1,
    st2, xr2, zs2, zr2, pb2, pf2,
    gg, gb, d1, d2, r1, r2, s1, s2, t1, t2, yb, yr,
    lsem, ssem, rsem,
):
    z, x, y, c = (lax.axis_index(a) for a in SEQ_BATCH)
    place = {"seq_0": z, "seq_1": x, "seq_2": y}
    started = []
    used = [0]

    def send(src, dst, target):
        k = used[0]
        used[0] += 1
        copy = pltpu.make_async_remote_copy(
            src_ref=src, dst_ref=dst, send_sem=ssem.at[k], recv_sem=rsem.at[k],
            device_id=target, device_id_type=MESH_ID,
        )
        copy.start()
        started.append(copy)
        return copy

    def at_peer(axis, d):
        return lax.rem(place[axis] + d, N)

    loads = {}

    def load(name, k, src, dst):
        loads[name] = pltpu.make_async_copy(src, dst, lsem.at[k])
        loads[name].start()

    load("x", 0, x_hbm.at[0], xb)
    load("wq", 1, wq_hbm, wq)
    load("wk", 2, wk_hbm, wk)
    for k, dy in enumerate(ORDER):
        cols = pl.ds(pl.multiple_of(at_peer("seq_2", dy) * 256, 256), 256)
        load(("wv", k), 3 + k, wv_hbm.at[:, cols], wv.at[k])
    load("u", 7, u_hbm.at[0], ub)

    barrier = pltpu.get_barrier_semaphore()
    for axis in SEQ:
        for d in (1, 2, 3):
            pl.semaphore_signal(
                barrier, inc=1, device_id={axis: at_peer(axis, d)}, device_id_type=MESH_ID
            )
    pl.semaphore_signal(barrier, inc=1, device_id={"batch": 1 - c}, device_id_type=MESH_ID)

    loads["x"].wait()
    loads["wq"].wait()
    qt = mm(xb[...], wq[...]).T
    loads["wk"].wait()
    kt = mm(xb[...], wk[...]).T
    for p in range(N):
        sqk[p, 0:32] = qt[32 * p : 32 * p + 32]
        sqk[p, 32:64] = kt[32 * p : 32 * p + 32]
    pl.semaphore_wait(barrier, 10)
    qk_in = []
    for dy in (1, 3, 2):
        p = at_peer("seq_2", dy)
        qk_in.append(send(sqk.at[p], rqk.at[y], {"seq_2": p}))
    rqk[y] = sqk[y]
    v_in = []
    for k, dy in enumerate(ORDER):
        p = at_peer("seq_2", dy)
        loads[("wv", k)].wait()
        v = mm(xb[...], wv[k]).astype(bf16).astype(f32)
        if dy:
            sv[k] = v
            v_in.append(send(sv.at[k], rv.at[y], {"seq_2": p}))
        else:
            rv[y] = v
    loads["u"].wait()
    for p in range(N):
        us[p] = ub[:, 256 * p : 256 * p + 256].astype(f32)
    u_in = []
    for dy in (1, 3, 2):
        p = at_peer("seq_2", dy)
        u_in.append(send(us.at[p], ur.at[y], {"seq_2": p}))
    ur[y] = us[y]

    for b in range(16):
        block = xb[:, 128 * b : 128 * b + 128].astype(f32).T
        for i in range(8):
            row = 64 * b + 16 * (i // 2)
            xt2[i % 2, row : row + 16] = block[16 * i : 16 * i + 16]
    pair_x = send(xt2.at[1 - c], xg.at[y, c], {"batch": 1 - c})
    xg[y, c] = xt2[c]

    for copy in qk_in:
        copy.wait_recv()
    us_q, us_k = [], []
    for h in range(2):
        lo = 16 * h
        uq = jnp.concatenate([rqk[j, lo : lo + 16] for j in range(N)], 1) * 0.5
        uk = jnp.concatenate([rqk[j, 32 + lo : 48 + lo] for j in range(N)], 1) * 0.5
        fq[h] = features(uq)
        fk[h] = features(uk)
    for copy in v_in:
        copy.wait_recv()
    ones = jnp.ones((16, TOK), bf16)
    for h in range(2):
        for j in range(N):
            vb[h, 128 * j : 128 * j + 128] = rv[j, :, 128 * h : 128 * h + 128].astype(bf16)

    def put_state(st, h, state, norm):
        st[2 * h] = state[:80]
        st[2 * h + 1] = state[80:]
        st[2 * h + 1, 73:74] = norm[:, :128]
        st[2 * h + 1, 74:75] = jnp.concatenate([norm[:, 128:], jnp.zeros((1, 96), f32)], 1)

    def get_state(pf, h):
        state = jnp.concatenate([pf[2 * h], pf[2 * h + 1]], 0)
        norm = jnp.concatenate([pf[2 * h + 1, 73:74], pf[2 * h + 1, 74:75, :32]], 1)
        return state, norm

    for h in range(2):
        put_state(st1, h, mm(fk[h], vb[h]), mm_nt(ones, fk[h])[:1])

    def scan_start(st, xr):
        copies = []
        for d in (1, 3, 2):
            p = at_peer("seq_1", d)
            copies.append(send(st.at[p], xr.at[x], {"seq_1": p}))
        xr[x] = st[x]
        return copies

    def scan_mid(copies, xr, zs, zr):
        for copy in copies:
            copy.wait_recv()
        zs[...] = (xr[0] + xr[1]) + (xr[2] + xr[3])
        return [send(zs, zr.at[z], {"seq_0": at_peer("seq_0", d)}) for d in (1, 3, 2)]

    def scan_back(copies, xr, zr, pb, pf, later):
        for copy in copies:
            copy.wait_recv()
        run = jnp.zeros((80, 128), f32)
        for d in (1, 2, 3):
            p = at_peer("seq_0", d)
            run = run + jnp.where(p > z if later else p < z, zr[p], 0.0)
        for i in reversed(range(N)) if later else range(N):
            pb[i] = run
            run = run + xr[i]
        out = []
        for d in (1, 3, 2):
            p = at_peer("seq_1", d)
            out.append(send(pb.at[p], pf.at[x], {"seq_1": p}))
        pf[x] = pb[x]
        return out

    keep = lax.broadcasted_iota(jnp.int32, (TOK, TOK), 1) >= lax.broadcasted_iota(
        jnp.int32, (TOK, TOK), 0
    )

    def local_forward(h):
        for j in range(N):
            vt[h, :, 128 * j : 128 * j + 128] = (
                rv[j, :, 128 * h : 128 * h + 128].T.astype(bf16)
            )
        scores = jnp.where(keep, mm_tn(fk[h], fq[h]), 0.0)
        dloc[h] = jnp.broadcast_to(jnp.sum(scores, 0, keepdims=True), (8, TOK))
        at[h] = scores.astype(bf16)
        num[h] = mm(vt[h], at[h])

    move = scan_start(st1, xr1)
    local_forward(0)
    move = scan_mid(move, xr1, zs1, zr1)
    local_forward(1)
    move = scan_back(move, xr1, zr1, pb1, pf1, False)
    pair_x.wait_recv()
    x_in = []
    for dy in (1, 3, 2):
        x_in.append(send(xg.at[y], xg.at[y], {"seq_2": at_peer("seq_2", dy)}))
    for copy in u_in:
        copy.wait_recv()
    for h in range(2):
        for j in range(N):
            ut[h, :, 128 * j : 128 * j + 128] = ur[j, :, 128 * h : 128 * h + 128].T
    for copy in move:
        copy.wait_recv()

    for h in range(2):
        state, norm = get_state(pf1, h)
        stb[h] = state.astype(bf16)
        n_hi, n_lo = halves(norm)
        nrm[h] = jnp.concatenate([n_hi, n_lo, n_hi, jnp.zeros((5, FP), f32)], 0)
        numer = num[h] + mm_tn(stb[h], fq[h])
        denom = dloc[h, :1] + jnp.sum(mm(rows16(n_hi, n_lo), fq[h]), 0, keepdims=True)
        inverse = 1.0 / denom
        upstream = ut[h]
        g_num = upstream * inverse
        g_den = -jnp.sum(upstream * (numer * inverse), 0, keepdims=True) * inverse
        gnb[h] = g_num.astype(bf16)
        g_hi, g_lo = halves(g_den)
        gdr[h] = jnp.concatenate([g_hi, g_lo, jnp.zeros((6, TOK), f32)], 0)
        back = mm_nt(fq[h], gnb[h])
        back_norm = jnp.sum(mm_nt(rows16(g_hi, g_lo), fq[h]), 0, keepdims=True)
        put_state(st2, h, back, back_norm)

    def local_backward(h):
        g_hi, g_lo = gdr[h, 0:1], gdr[h, 1:2]
        n_hi, n_lo = nrm[h, 0:1], nrm[h, 1:2]
        inner = mm(vb[h], gnb[h]) + (g_hi + g_lo)
        ga = jnp.where(keep, inner, 0.0).astype(bf16)
        outer = mm_tn(rows16(n_hi, n_lo, n_hi), rows16(g_hi, g_hi, g_lo))
        gfq[h] = mm(fk[h], ga) + mm(stb[h], gnb[h]) + outer
        gvt[h] = mm_nt(gnb[h], at[h])
        gfk[h] = mm_nt(fq[h], ga)

    def put_grad(h, first, u, grad):
        out = (pull_back(u, grad) * 0.5).astype(bf16).astype(f32)
        for j in range(N):
            gg[c, j, first + 16 * h : first + 16 * h + 16] = out[:, 128 * j : 128 * j + 128]

    move = scan_start(st2, xr2)
    local_backward(0)
    move = scan_mid(move, xr2, zs2, zr2)
    local_backward(1)
    move = scan_back(move, xr2, zr2, pb2, pf2, True)
    for h in range(2):
        lo = 16 * h
        uq = jnp.concatenate([rqk[j, lo : lo + 16] for j in range(N)], 1) * 0.5
        put_grad(h, 256, uq, gfq[h])
    for copy in move:
        copy.wait_recv()
    first16 = lax.broadcasted_iota(jnp.int32, (16, TOK), 0) < 2
    flag = jnp.where(first16, 1.0, 0.0).astype(bf16)
    for h in range(2):
        back, back_norm = get_state(pf2, h)
        backb = back.astype(bf16)
        b_hi, b_lo = halves(back_norm)
        g_val = gvt[h] + mm_tn(backb, fk[h])
        g_val = g_val.astype(bf16).astype(f32)
        for j in range(N):
            gg[c, j, 128 * h : 128 * h + 128] = g_val[:, 128 * j : 128 * j + 128]
        g_fk = gfk[h] + mm(backb, vt[h]) + mm_tn(rows16(b_hi, b_lo), flag)
        lo = 32 + 16 * h
        uk = jnp.concatenate([rqk[j, lo : lo + 16] for j in range(N)], 1) * 0.5
        put_grad(h, 288, uk, g_fk)

    pair_g = send(gg.at[c], gg.at[c], {"batch": 1 - c})
    g_in = []
    for dy in (1, 3, 2):
        p = at_peer("seq_2", dy)
        g_in.append(send(gg.at[c, p], gb.at[y], {"seq_2": p}))
    gb[y] = gg[c, y]

    pair_g.wait_recv()
    for copy in x_in:
        copy.wait_recv()
    rhs = jnp.concatenate([gg[i, j].astype(bf16) for j in range(N) for i in range(2)], 1)

    def weights_of(zz, carry):
        rows = pl.ds(pl.multiple_of(zz * 256, 256), 256)
        lhs = jnp.concatenate([xg[j, i, rows].astype(bf16) for j in range(N) for i in range(2)], 1)
        part = mm_nt(lhs, rhs)
        for xx in range(N):
            own = part[64 * xx : 64 * xx + 64]
            thin = own[:, 256:320]
            thin = jnp.concatenate([thin[:32], thin[32:]], 1)
            d1[xx, zz, 0:64] = own[:, :128]
            d1[xx, zz, 64:80] = own[:16, 128:256]
            d2[zz, xx, 0:48] = own[16:, 128:256]
            d2[zz, xx, 48:80] = thin
        return carry

    lax.fori_loop(0, N, weights_of, 0)

    far1, far2 = [], []
    for i, d in enumerate((1, 3, 2)):
        p = at_peer("seq_1", d)
        far1.append(send(d1.at[p], r1.at[i], {"seq_1": p}))
        p = at_peer("seq_0", d)
        far2.append(send(d2.at[p], r2.at[i], {"seq_0": p}))

    for copy in g_in:
        copy.wait_recv()
    g_q = jnp.concatenate([gb[j, 256:288] for j in range(N)], 0).T.astype(bf16)
    g_k = jnp.concatenate([gb[j, 288:320] for j in range(N)], 0).T.astype(bf16)
    g_v = []
    for k, dy in enumerate(ORDER):
        p = at_peer("seq_2", dy)
        g_v.append(gb[p, 0:256].T.astype(bf16))

    def inputs_of(i, carry):
        rows = pl.ds(pl.multiple_of(i * 512, 512), 512)
        acc = mm_nt(g_q, wq[rows]) + mm_nt(g_k, wk[rows])
        for k in range(N):
            acc = acc + mm_nt(g_v[k], wv[k, rows])
        gin[0, :, rows] = acc.astype(bf16)
        return carry

    lax.fori_loop(0, N, inputs_of, 0)

    for copy in far1:
        copy.wait_recv()
    s1[...] = (d1[x] + r1[0]) + (r1[1] + r1[2])
    near1 = []
    for i, d in enumerate((1, 3, 2)):
        p = at_peer("seq_0", d)
        near1.append(send(s1.at[p], t1.at[i], {"seq_0": p}))
    for copy in far2:
        copy.wait_recv()
    s2[...] = (d2[z] + r2[0]) + (r2[1] + r2[2])
    near2 = []
    for i, d in enumerate((1, 3, 2)):
        p = at_peer("seq_1", d)
        near2.append(send(s2.at[p], t2.at[i], {"seq_1": p}))
    for copy in near1:
        copy.wait_recv()
    one = (s1[z] + t1[0]) + (t1[1] + t1[2])
    for copy in near2:
        copy.wait_recv()
    two = (s2[x] + t2[0]) + (t2[1] + t2[2])
    for j in range(N):
        yb[j, 0:16] = one[16 * j : 16 * j + 16]
        yb[j, 16:32] = one[64:80] if j == 0 else two[16 * j - 16 : 16 * j]
        yb[j, 32:48] = two[48 + 16 * (j % 2) : 64 + 16 * (j % 2)]
    y_in = []
    for dy in (1, 3, 2):
        p = at_peer("seq_2", dy)
        y_in.append(send(yb.at[p], yr.at[y], {"seq_2": p}))
    yr[y] = yb[y]
    for copy in y_in:
        copy.wait_recv()
    lane = lax.broadcasted_iota(jnp.int32, (16, 128), 1) // 32
    w_q = jnp.zeros((16, 128), f32)
    w_k = jnp.zeros((16, 128), f32)
    for p in range(N):
        gwv[:, 256 * p : 256 * p + 128] = yr[p, 0:16]
        gwv[:, 256 * p + 128 : 256 * p + 256] = yr[p, 16:32]
        thin = yr[p, 32:48]
        thin = jnp.where(y >= 2, pltpu.roll(thin, 64, 1), thin)
        from_q = pltpu.roll(thin, 32 * p, 1) if p else thin
        w_q = jnp.where(lane == p, from_q, w_q)
        from_k = pltpu.roll(thin, (32 * p + 96) % 128, 1) if p != 1 else thin
        w_k = jnp.where(lane == p, from_k, w_k)
    gwq[...] = w_q
    gwk[...] = w_k
    for copy in started:
        copy.wait_send()


SENDS = 1 + 3 + 3 + 3 + 3 + 9 + 9 + 1 + 3 + 6 + 6 + 3


def body(inputs, cotangent, w_query, w_key, w_value):
    vmem = pltpu.VMEM
    hbm = pl.BlockSpec(memory_space=pl.ANY)
    here = pl.BlockSpec(memory_space=pltpu.VMEM)
    scan = [
        vmem((4, 80, 128), f32), vmem((4, 80, 128), f32), vmem((80, 128), f32),
        vmem((4, 80, 128), f32), vmem((4, 80, 128), f32), vmem((4, 80, 128), f32),
    ]
    scratch = [
        vmem((BLK, D), bf16), vmem((BLK, 1024), bf16), vmem((D, 128), bf16), vmem((D, 128), bf16),
        vmem((4, D, 256), bf16), vmem((2, 1024, 128), f32), vmem((4, 2, 1024, 128), f32),
        vmem((4, 64, 128), f32), vmem((3, 128, 256), f32), vmem((4, 64, 128), f32),
        vmem((4, 128, 256), f32), vmem((4, 128, 256), f32), vmem((4, 128, 256), f32),
        vmem((2, FP, TOK), bf16), vmem((2, FP, TOK), bf16), vmem((2, TOK, 128), bf16),
        vmem((2, 128, TOK), bf16), vmem((2, 128, TOK), f32), vmem((2, TOK, TOK), bf16),
        vmem((2, 128, TOK), f32), vmem((2, 8, TOK), f32), vmem((2, 128, TOK), bf16),
        vmem((2, 8, TOK), f32), vmem((2, FP, TOK), f32), vmem((2, FP, TOK), f32),
        vmem((2, 128, TOK), f32), vmem((2, FP, 128), bf16), vmem((2, 8, FP), f32),
        *scan, *scan,
        vmem((2, 4, 320, 128), f32), vmem((4, 320, 128), f32),
        vmem((4, 4, 80, 128), f32), vmem((4, 4, 80, 128), f32),
        vmem((3, 4, 80, 128), f32), vmem((3, 4, 80, 128), f32),
        vmem((4, 80, 128), f32), vmem((4, 80, 128), f32),
        vmem((3, 80, 128), f32), vmem((3, 80, 128), f32),
        vmem((4, 48, 128), f32), vmem((4, 48, 128), f32),
        pltpu.SemaphoreType.DMA((8,)), pltpu.SemaphoreType.DMA((SENDS,)),
        pltpu.SemaphoreType.DMA((SENDS,)),
    ]
    return pl.pallas_call(
        kernel,
        out_shape=(
            jax.ShapeDtypeStruct((1, BLK, D), bf16),
            jax.ShapeDtypeStruct((16, 128), f32),
            jax.ShapeDtypeStruct((16, 128), f32),
            jax.ShapeDtypeStruct((16, 1024), f32),
        ),
        in_specs=[hbm] * 5,
        out_specs=(here,) * 4,
        scratch_shapes=scratch,
        compiler_params=pltpu.CompilerParams(
            collective_id=0, has_side_effects=True, vmem_limit_bytes=60 * 1024 * 1024
        ),
    )(inputs, cotangent, w_query, w_key, w_value)


def solution(mesh):
    split = Mesh(
        mesh.devices.reshape(4, 4, 4, mesh.shape["batch"]), ("seq_0", "seq_1", "seq_2", "batch")
    )
    in_specs = (P("batch", SEQ, None), P("batch", SEQ, None), P(), P(), P())
    out_specs = (P("batch", SEQ, None), P(SEQ_BATCH, None), P(SEQ_BATCH, None), P(SEQ_BATCH, None))
    return jax.shard_map(body, mesh=split, in_specs=in_specs, out_specs=out_specs, check_vma=False)
```

time: 416 us -> 101 us (0.24)
  waiting for transfers between devices: 229 us -> 0 us
  Pallas kernels: 0 us -> 93.7 us
  blocking collectives: 88.3 us -> 0 us
  matrix products: 33.8 us -> 0 us
  other arithmetic: 24.8 us -> 0 us
  local copies, waits for them, and re-layouts: 23.9 us -> 5.94 us
  between operations: 14.5 us -> 0.64 us
    all_gather x6 -> x0, waiting for transfers between devices: 130 us -> none  [entering(): pieces = jax.tree.map(lambda part: lax.all_gather(part, axis), total)]
    reduce_scatter x3 -> x0, waiting for transfers between devices: 98.7 us -> none  [scatter_axes(): shard = lax.psum_scatter(shard, axis, scatter_dimension=dim, tiled=True)]
    pallas_call x0 -> x1, Pallas kernels: none -> 93.7 us  [body(): pl.pallas_call(kernel, out_shape=(jax.ShapeDtypeStruct((1, BLK, D), bf16)...]
    all_gather x6 -> x0, blocking collectives: 74.7 us -> none  [entering(): pieces = jax.tree.map(lambda part: lax.all_gather(part, axis), total)]
    dot_general x29 -> x0, matrix products: 33.8 us -> none  [the longest x1 5.54 us: body(): lax.dot_general(tokens, joined_grads, (((0,), (0,)), ((), ())), preferred...]
    add x13 -> x0, other arithmetic: 16.4 us -> none  [the longest x11 16.4 us: add_pair(): return (earlier[0] + later[0], earlier[1] + later[1])]
    dot_general x4 -> x0, local copies, waits for them, and re-layouts: 13.7 us -> none  [the longest x1 11.2 us: body(): lax.dot_general(tokens, joined_grads, (((0,), (0,)), ((), ())), preferred...]
    all_to_all x1 -> x0, blocking collectives: 13.6 us -> none  [summed_on_arrival(): lax.all_to_all(pieces, axis, split_axis=0, concat_axis=0, tiled=True)]
  transfers between devices with their start and end apart: 9 -> 0, of which waited for: 7 -> 0; matrix products, arithmetic and copies ran while one was open for 8% -> 0% of each run, Pallas kernels for 0% -> 0%
where the time goes in v1:
time: 101 us; the launch traced here: 100 us
  Pallas kernels  93.7 us (93%)
  local copies, waits for them, and re-layouts  5.94 us (6%)
    pallas_call x1, Pallas kernels, body(): pl.pallas_call(kernel, out_shape=(jax.ShapeDtypeStruct((1, BLK, D), bf16)...  93.7 us
    unnamed x4, local copies, waits for them, and re-layouts  5.94 us

profile of v1, /device:TPU:0, one launch (start us, length us, event | category | flops | bytes accessed | tf_op | source)
XLA Modules:
  0.0 100.3 jit_solution(11868894383904429197)
XLA Ops:
  0.6 93.7 %shard_map.84 = (bf16[1,128,2048]{2,1,0:T(8,128)(2,1)}, f32[16,128]{1,0:T(8,128)}, f32[16,128]{1,0:T(8,128)}, f32[16,1024]{1,0:T(8,128)}) custom-call(bf16[1,128,2048]{2,1,0:T(8,128)(2,1)} %x_hbm.1, bf16[1,128,1024]{2,1,0:T(8,128)(2,1)} %u_hbm.1, bf16[2048,128]{1,0:T(8,128)(2,1)} %wq_hbm.1, bf16[2048,128]{1,0:T(8,128)(2,1)} %wk_hbm.1, bf16[2048,1024]{1,0:T(8,128)(2,1)} %wv_hbm.1), custom_call_target="tpu_custom_call" | custom-call | tf_op jit(solution)/shard_map/pallas_call | solution.py:457
  94.3 1.9 %copy.13 = bf16[1,128,2048]{2,1,0:T(8,128)(2,1)} copy(bf16[1,128,2048]{2,1,0:T(8,128)(2,1)} %get-tuple-element.8) | data formatting | bytes 1048576
  96.2 1.3 %copy.14 = f32[16,128]{1,0:T(8,128)} copy(f32[16,128]{1,0:T(8,128)} %get-tuple-element.9) | data formatting | bytes 16384
  97.5 1.3 %copy.15 = f32[16,128]{1,0:T(8,128)} copy(f32[16,128]{1,0:T(8,128)} %get-tuple-element.10) | data formatting | bytes 16384
  98.8 1.5 %copy.16 = f32[16,1024]{1,0:T(8,128)} copy(f32[16,1024]{1,0:T(8,128)} %get-tuple-element.11) | data formatting | bytes 131072

commit v2 on v1

--- a/solution.py
+++ b/solution.py
@@ -78,14 +78,14 @@
 
 def kernel(
     x_hbm, u_hbm, wq_hbm, wk_hbm, wv_hbm,
-    gin, gwq, gwk, gwv,
+    gin, res,
     xb, ub, wq, wk, wv, xt2, xg,
     sqk, sv, rqk, rv, us, ur,
     fq, fk, vb, vt, ut, at, num, dloc, gnb, gdr, gfq, gfk, gvt, stb, nrm,
     st1, xr1, zs1, zr1, pb1, pf1,
     st2, xr2, zs2, zr2, pb2, pf2,
-    gg, gb, d1, d2, r1, r2, s1, s2, t1, t2, yb, yr,
-    lsem, ssem, rsem,
+    gg, gb, gi, da, db, ra, rb, sa, fa, fb,
+    lsem, osem, ssem, rsem,
 ):
     z, x, y, c = (lax.axis_index(a) for a in SEQ_BATCH)
     place = {"seq_0": z, "seq_1": x, "seq_2": y}
@@ -121,12 +121,23 @@
     load("u", 7, u_hbm.at[0], ub)
 
     barrier = pltpu.get_barrier_semaphore()
-    for axis in SEQ:
-        for d in (1, 2, 3):
-            pl.semaphore_signal(
-                barrier, inc=1, device_id={axis: at_peer(axis, d)}, device_id_type=MESH_ID
-            )
-    pl.semaphore_signal(barrier, inc=1, device_id={"batch": 1 - c}, device_id_type=MESH_ID)
+    greeted = 0
+    for d in range(N):
+        for e in range(N):
+            pairs = [("seq_0", "seq_2")] if d or e else []
+            if d:
+                pairs.append(("seq_1", "seq_2"))
+            for first, second in pairs:
+                greeted += 1
+                pl.semaphore_signal(
+                    barrier, inc=1, device_id_type=MESH_ID,
+                    device_id={first: at_peer(first, d), second: at_peer(second, e)},
+                )
+        greeted += 1
+        pl.semaphore_signal(
+            barrier, inc=1, device_id_type=MESH_ID,
+            device_id={"seq_2": at_peer("seq_2", d), "batch": 1 - c},
+        )
 
     loads["x"].wait()
     loads["wq"].wait()
@@ -136,7 +147,7 @@
     for p in range(N):
         sqk[p, 0:32] = qt[32 * p : 32 * p + 32]
         sqk[p, 32:64] = kt[32 * p : 32 * p + 32]
-    pl.semaphore_wait(barrier, 10)
+    pl.semaphore_wait(barrier, greeted)
     qk_in = []
     for dy in (1, 3, 2):
         p = at_peer("seq_2", dy)
@@ -164,14 +175,40 @@
     for b in range(16):
         block = xb[:, 128 * b : 128 * b + 128].astype(f32).T
         for i in range(8):
-            row = 64 * b + 16 * (i // 2)
-            xt2[i % 2, row : row + 16] = block[16 * i : 16 * i + 16]
-    pair_x = send(xt2.at[1 - c], xg.at[y, c], {"batch": 1 - c})
-    xg[y, c] = xt2[c]
+            row = 64 * (b % 4) + 16 * (i // 2)
+            xt2[i % 2, b // 4, row : row + 16] = block[16 * i : 16 * i + 16]
+    chunk = [lax.rem(z + i + 1, N) for i in range(N)]
+    after, before = at_peer("seq_2", 1), at_peer("seq_2", 3)
+    x_in = [[] for _ in range(N)]
+    passing = [None] * N
+
+    def x_start(i):
+        part = chunk[i]
+        mine = xg.at[part, y, c]
+        x_in[i].append(send(xt2.at[1 - c, part], mine, {"batch": 1 - c}))
+        same, cross = [], []
+        for p in (after, before):
+            same.append(send(xt2.at[c, part], mine, {"seq_2": p, "batch": c}))
+            cross.append(send(xt2.at[1 - c, part], mine, {"seq_2": p, "batch": 1 - c}))
+        xg[part, y, c] = xt2[c, part]
+        x_in[i] += [same[1], cross[0]]
+        passing[i] = (same[0], cross[1])
+
+    def x_pass(i):
+        part = chunk[i]
+        up, down = passing[i]
+        up.wait_recv()
+        move = xg.at[part, before, c]
+        x_in[i].append(send(move, move, {"seq_2": after}))
+        down.wait_recv()
+        move = xg.at[part, after, 1 - c]
+        x_in[i].append(send(move, move, {"seq_2": before}))
+
+    for i in range(N - 1):
+        x_start(i)
 
     for copy in qk_in:
         copy.wait_recv()
-    us_q, us_k = [], []
     for h in range(2):
         lo = 16 * h
         uq = jnp.concatenate([rqk[j, lo : lo + 16] for j in range(N)], 1) * 0.5
@@ -249,10 +286,6 @@
     move = scan_mid(move, xr1, zs1, zr1)
     local_forward(1)
     move = scan_back(move, xr1, zr1, pb1, pf1, False)
-    pair_x.wait_recv()
-    x_in = []
-    for dy in (1, 3, 2):
-        x_in.append(send(xg.at[y], xg.at[y], {"seq_2": at_peer("seq_2", dy)}))
     for copy in u_in:
         copy.wait_recv()
     for h in range(2):
@@ -295,8 +328,11 @@
             gg[c, j, first + 16 * h : first + 16 * h + 16] = out[:, 128 * j : 128 * j + 128]
 
     move = scan_start(st2, xr2)
+    x_pass(0)
+    x_start(3)
     local_backward(0)
     move = scan_mid(move, xr2, zs2, zr2)
+    x_pass(1)
     local_backward(1)
     move = scan_back(move, xr2, zr2, pb2, pf2, True)
     for h in range(2):
@@ -321,39 +357,79 @@
         put_grad(h, 288, uk, g_fk)
 
     pair_g = send(gg.at[c], gg.at[c], {"batch": 1 - c})
+    x_pass(2)
+    pair_g.wait_recv()
+    rhs = jnp.concatenate([gg[i, j].astype(bf16) for j in range(N) for i in range(2)], 1)
+
+    a_in, b_in = [], []
+
+    def weights_of(i):
+        part = chunk[i]
+        for copy in x_in[i]:
+            copy.wait_recv()
+        lhs = jnp.concatenate(
+            [xg[part, j, k].astype(bf16) for j in range(N) for k in range(2)], 1
+        )
+        out = mm_nt(lhs, rhs)
+        for xx in range(N):
+            for j in range(N):
+                own = out[64 * xx + 16 * j : 64 * xx + 16 * j + 16]
+                thin = own[:, 256:320]
+                da[i, xx, 24 * j : 24 * j + 16] = own[:, :128]
+                da[i, xx, 24 * j + 16 : 24 * j + 24] = jnp.concatenate([thin[:8], thin[8:]], 1)
+                db[i, xx, 16 * j : 16 * j + 16] = own[:, 128:256]
+        a_in.append([])
+        for k, d in enumerate((1, 3, 2)):
+            p = at_peer("seq_1", d)
+            a_in[i].append(send(da.at[i, p], ra.at[i, k], {"seq_1": p}))
+        if i < N - 1:
+            b_in.append(send(db.at[i], rb.at[i], {"seq_0": part}))
+
+    last = []
+
+    def a_onward(i):
+        for copy in a_in[i]:
+            copy.wait_recv()
+        total = (da[i, x] + ra[i, 0]) + (ra[i, 1] + ra[i, 2])
+        for j in range(N):
+            sa[i, j] = total[24 * j : 24 * j + 24]
+        for dy in ORDER:
+            p = at_peer("seq_2", dy)
+            target = {"seq_2": p}
+            if i < N - 1:
+                target["seq_0"] = chunk[i]
+            elif dy == 0:
+                fa[i, y] = sa[i, y]
+                continue
+            last.append(send(sa.at[i, p], fa.at[i, y], target))
+
+    weights_of(0)
+    weights_of(1)
+    a_onward(0)
+    weights_of(2)
+    x_pass(3)
     g_in = []
     for dy in (1, 3, 2):
         p = at_peer("seq_2", dy)
         g_in.append(send(gg.at[c, p], gb.at[y], {"seq_2": p}))
     gb[y] = gg[c, y]
-
-    pair_g.wait_recv()
-    for copy in x_in:
-        copy.wait_recv()
-    rhs = jnp.concatenate([gg[i, j].astype(bf16) for j in range(N) for i in range(2)], 1)
-
-    def weights_of(zz, carry):
-        rows = pl.ds(pl.multiple_of(zz * 256, 256), 256)
-        lhs = jnp.concatenate([xg[j, i, rows].astype(bf16) for j in range(N) for i in range(2)], 1)
-        part = mm_nt(lhs, rhs)
-        for xx in range(N):
-            own = part[64 * xx : 64 * xx + 64]
-            thin = own[:, 256:320]
-            thin = jnp.concatenate([thin[:32], thin[32:]], 1)
-            d1[xx, zz, 0:64] = own[:, :128]
-            d1[xx, zz, 64:80] = own[:16, 128:256]
-            d2[zz, xx, 0:48] = own[16:, 128:256]
-            d2[zz, xx, 48:80] = thin
-        return carry
-
-    lax.fori_loop(0, N, weights_of, 0)
-
-    far1, far2 = [], []
-    for i, d in enumerate((1, 3, 2)):
-        p = at_peer("seq_1", d)
-        far1.append(send(d1.at[p], r1.at[i], {"seq_1": p}))
-        p = at_peer("seq_0", d)
-        far2.append(send(d2.at[p], r2.at[i], {"seq_0": p}))
+    a_onward(1)
+    a_onward(2)
+    weights_of(3)
+    for copy in b_in:
+        copy.wait_recv()
+    for xx in range(N):
+        db[3, xx] = (db[3, xx] + rb[0, xx]) + (rb[1, xx] + rb[2, xx])
+    for d in ORDER:
+        px = at_peer("seq_1", d)
+        for dy in ORDER:
+            p = at_peer("seq_2", dy)
+            piece = db.at[3, px, pl.ds(pl.multiple_of(p * 16, 16), 16)]
+            if d or dy:
+                last.append(send(piece, fb.at[d, y], {"seq_1": px, "seq_2": p}))
+            else:
+                fb[0, y] = piece[...]
+    a_onward(3)
 
     for copy in g_in:
         copy.wait_recv()
@@ -369,61 +445,44 @@
         acc = mm_nt(g_q, wq[rows]) + mm_nt(g_k, wk[rows])
         for k in range(N):
             acc = acc + mm_nt(g_v[k], wv[k, rows])
-        gin[0, :, rows] = acc.astype(bf16)
+        gi[:, rows] = acc.astype(bf16)
         return carry
 
     lax.fori_loop(0, N, inputs_of, 0)
-
-    for copy in far1:
-        copy.wait_recv()
-    s1[...] = (d1[x] + r1[0]) + (r1[1] + r1[2])
-    near1 = []
-    for i, d in enumerate((1, 3, 2)):
-        p = at_peer("seq_0", d)
-        near1.append(send(s1.at[p], t1.at[i], {"seq_0": p}))
-    for copy in far2:
-        copy.wait_recv()
-    s2[...] = (d2[z] + r2[0]) + (r2[1] + r2[2])
-    near2 = []
-    for i, d in enumerate((1, 3, 2)):
-        p = at_peer("seq_1", d)
-        near2.append(send(s2.at[p], t2.at[i], {"seq_1": p}))
-    for copy in near1:
-        copy.wait_recv()
-    one = (s1[z] + t1[0]) + (t1[1] + t1[2])
-    for copy in near2:
-        copy.wait_recv()
-    two = (s2[x] + t2[0]) + (t2[1] + t2[2])
-    for j in range(N):
-        yb[j, 0:16] = one[16 * j : 16 * j + 16]
-        yb[j, 16:32] = one[64:80] if j == 0 else two[16 * j - 16 : 16 * j]
-        yb[j, 32:48] = two[48 + 16 * (j % 2) : 64 + 16 * (j % 2)]
-    y_in = []
-    for dy in (1, 3, 2):
-        p = at_peer("seq_2", dy)
-        y_in.append(send(yb.at[p], yr.at[y], {"seq_2": p}))
-    yr[y] = yb[y]
-    for copy in y_in:
-        copy.wait_recv()
+    out_copy = pltpu.make_async_copy(gi, gin.at[0], osem)
+    out_copy.start()
+    for copy in last:
+        copy.wait_recv()
+    for p in range(N):
+        both = (fa[0, p] + fa[1, p]) + (fa[2, p] + fa[3, p])
+        res[p, 0:16] = both[:16]
+        res[p, 16:32] = (fb[0, p] + fb[1, p]) + (fb[2, p] + fb[3, p])
+        res[p, 32:40] = both[16:]
+    out_copy.wait()
+    assert used[0] == SENDS
+    for copy in started:
+        copy.wait_send()
+
+
+def finish(gin_ref, res_ref, gin_out, gwq, gwk, gwv):
+    gin_out[...] = gin_ref[...]
     lane = lax.broadcasted_iota(jnp.int32, (16, 128), 1) // 32
     w_q = jnp.zeros((16, 128), f32)
     w_k = jnp.zeros((16, 128), f32)
     for p in range(N):
-        gwv[:, 256 * p : 256 * p + 128] = yr[p, 0:16]
-        gwv[:, 256 * p + 128 : 256 * p + 256] = yr[p, 16:32]
-        thin = yr[p, 32:48]
-        thin = jnp.where(y >= 2, pltpu.roll(thin, 64, 1), thin)
+        gwv[:, 256 * p : 256 * p + 128] = res_ref[p, 0:16]
+        gwv[:, 256 * p + 128 : 256 * p + 256] = res_ref[p, 16:32]
+        thin = res_ref[p, 32:40]
+        thin = jnp.concatenate([thin, pltpu.roll(thin, 64, 1)], 0)
         from_q = pltpu.roll(thin, 32 * p, 1) if p else thin
         w_q = jnp.where(lane == p, from_q, w_q)
         from_k = pltpu.roll(thin, (32 * p + 96) % 128, 1) if p != 1 else thin
         w_k = jnp.where(lane == p, from_k, w_k)
     gwq[...] = w_q
     gwk[...] = w_k
-    for copy in started:
-        copy.wait_send()
-
-
-SENDS = 1 + 3 + 3 + 3 + 3 + 9 + 9 + 1 + 3 + 6 + 6 + 3
+
+
+SENDS = 3 + 3 + 3 + 18 + 1 + 4 * 7 + 3 + 12 + 3 + 15 + 15
 
 
 def body(inputs, cotangent, w_query, w_key, w_value):
@@ -436,7 +495,7 @@
     ]
     scratch = [
         vmem((BLK, D), bf16), vmem((BLK, 1024), bf16), vmem((D, 128), bf16), vmem((D, 128), bf16),
-        vmem((4, D, 256), bf16), vmem((2, 1024, 128), f32), vmem((4, 2, 1024, 128), f32),
+        vmem((4, D, 256), bf16), vmem((2, 4, 256, 128), f32), vmem((4, 4, 2, 256, 128), f32),
         vmem((4, 64, 128), f32), vmem((3, 128, 256), f32), vmem((4, 64, 128), f32),
         vmem((4, 128, 256), f32), vmem((4, 128, 256), f32), vmem((4, 128, 256), f32),
         vmem((2, FP, TOK), bf16), vmem((2, FP, TOK), bf16), vmem((2, TOK, 128), bf16),
@@ -445,30 +504,37 @@
         vmem((2, 8, TOK), f32), vmem((2, FP, TOK), f32), vmem((2, FP, TOK), f32),
         vmem((2, 128, TOK), f32), vmem((2, FP, 128), bf16), vmem((2, 8, FP), f32),
         *scan, *scan,
-        vmem((2, 4, 320, 128), f32), vmem((4, 320, 128), f32),
-        vmem((4, 4, 80, 128), f32), vmem((4, 4, 80, 128), f32),
-        vmem((3, 4, 80, 128), f32), vmem((3, 4, 80, 128), f32),
-        vmem((4, 80, 128), f32), vmem((4, 80, 128), f32),
-        vmem((3, 80, 128), f32), vmem((3, 80, 128), f32),
-        vmem((4, 48, 128), f32), vmem((4, 48, 128), f32),
-        pltpu.SemaphoreType.DMA((8,)), pltpu.SemaphoreType.DMA((SENDS,)),
+        vmem((2, 4, 320, 128), f32), vmem((4, 320, 128), f32), vmem((BLK, D), bf16),
+        vmem((4, 4, 96, 128), f32), vmem((4, 4, 64, 128), f32),
+        vmem((4, 3, 96, 128), f32), vmem((3, 4, 64, 128), f32),
+        vmem((4, 4, 24, 128), f32), vmem((4, 4, 24, 128), f32), vmem((4, 4, 16, 128), f32),
+        pltpu.SemaphoreType.DMA((8,)), pltpu.SemaphoreType.DMA, pltpu.SemaphoreType.DMA((SENDS,)),
         pltpu.SemaphoreType.DMA((SENDS,)),
     ]
+    gin, res = pl.pallas_call(
+        kernel,
+        out_shape=(
+            jax.ShapeDtypeStruct((1, BLK, D), bf16),
+            jax.ShapeDtypeStruct((4, 40, 128), f32),
+        ),
+        in_specs=[hbm] * 5,
+        out_specs=(hbm, here),
+        scratch_shapes=scratch,
+        compiler_params=pltpu.CompilerParams(
+            collective_id=0, has_side_effects=True, vmem_limit_bytes=60 * 1024 * 1024
+        ),
+    )(inputs, cotangent, w_query, w_key, w_value)
     return pl.pallas_call(
-        kernel,
+        finish,
         out_shape=(
             jax.ShapeDtypeStruct((1, BLK, D), bf16),
             jax.ShapeDtypeStruct((16, 128), f32),
             jax.ShapeDtypeStruct((16, 128), f32),
             jax.ShapeDtypeStruct((16, 1024), f32),
         ),
-        in_specs=[hbm] * 5,
+        in_specs=[here] * 2,
         out_specs=(here,) * 4,
-        scratch_shapes=scratch,
-        compiler_params=pltpu.CompilerParams(
-            collective_id=0, has_side_effects=True, vmem_limit_bytes=60 * 1024 * 1024
-        ),
-    )(inputs, cotangent, w_query, w_key, w_value)
+    )(gin, res)
 
 
 def solution(mesh):

time: 101 us -> 75.8 us (0.75)
  Pallas kernels: 93.7 us -> 75 us
  local copies, waits for them, and re-layouts: 5.94 us -> 0 us
    pallas_call x1, Pallas kernels: 93.7 us -> 73.1 us  [body(): pl.pallas_call(kernel, out_shape=(jax.ShapeDtypeStruct((1, BLK, D), bf16)...]
    unnamed x4 -> x0, local copies, waits for them, and re-layouts: 5.94 us -> none
    pallas_call x0 -> x1, Pallas kernels: none -> 1.93 us  [body(): pl.pallas_call(finish, out_shape=(jax.ShapeDtypeStruct((1, BLK, D), bf16)...]
where the time goes in v2:
time: 75.8 us; the launch traced here: 75.6 us
  Pallas kernels  75 us (99%)
    pallas_call x1, Pallas kernels, body(): pl.pallas_call(kernel, out_shape=(jax.ShapeDtypeStruct((1, BLK, D), bf16)...  73.1 us
    pallas_call x1, Pallas kernels, body(): pl.pallas_call(finish, out_shape=(jax.ShapeDtypeStruct((1, BLK, D), bf16)...  1.93 us

profile of v2, /device:TPU:0, one launch (start us, length us, event | category | flops | bytes accessed | tf_op | source)
XLA Modules:
  0.0 75.6 jit_solution(13670993830340001274)
XLA Ops:
  0.6 73.1 %shard_map.84 = (bf16[1,128,2048]{2,1,0:T(8,128)(2,1)}, f32[4,40,128]{2,1,0:T(8,128)}) custom-call(bf16[1,128,2048]{2,1,0:T(8,128)(2,1)} %x_hbm.1, bf16[1,128,1024]{2,1,0:T(8,128)(2,1)} %u_hbm.1, bf16[2048,128]{1,0:T(8,128)(2,1)} %wq_hbm.1, bf16[2048,128]{1,0:T(8,128)(2,1)} %wk_hbm.1, bf16[2048,1024]{1,0:T(8,128)(2,1)} %wv_hbm.1), custom_call_target="tpu_custom_call" | custom-call | tf_op jit(solution)/shard_map/pallas_call | solution.py:514
  73.7 1.9 %shard_map.85 = (bf16[1,128,2048]{2,1,0:T(8,128)(2,1)}, f32[16,128]{1,0:T(8,128)}, f32[16,128]{1,0:T(8,128)}, f32[16,1024]{1,0:T(8,128)}) custom-call(bf16[1,128,2048]{2,1,0:T(8,128)(2,1)} %get-tuple-element.6.gin_ref, f32[4,40,128]{2,1,0:T(8,128)} %get-tuple-element.7.res_ref), custom_call_target="tpu_custom_call" | custom-call | tf_op jit(solution)/shard_map/pallas_call | solution.py:527

commit v3 on v2

--- a/solution.py
+++ b/solution.py
@@ -84,24 +84,38 @@
     fq, fk, vb, vt, ut, at, num, dloc, gnb, gdr, gfq, gfk, gvt, stb, nrm,
     st1, xr1, zs1, zr1, pb1, pf1,
     st2, xr2, zs2, zr2, pb2, pf2,
-    gg, gb, gi, da, db, ra, rb, sa, fa, fb,
-    lsem, osem, ssem, rsem,
+    gg, gb, gi, gacc, da, db, ra, rb, sa, fa, fb, rs, total,
+    lsem, osem, rsm, ssem, rsem,
 ):
     z, x, y, c = (lax.axis_index(a) for a in SEQ_BATCH)
     place = {"seq_0": z, "seq_1": x, "seq_2": y}
-    started = []
-    used = [0]
-
-    def send(src, dst, target):
-        k = used[0]
-        used[0] += 1
-        copy = pltpu.make_async_remote_copy(
-            src_ref=src, dst_ref=dst, send_sem=ssem.at[k], recv_sem=rsem.at[k],
-            device_id=target, device_id_type=MESH_ID,
-        )
-        copy.start()
-        started.append(copy)
-        return copy
+    bytes_sent, groups = [0], [0]
+
+    class Group:
+        def __init__(self, like):
+            self.like, self.k = like, groups[0]
+            groups[0] += 1
+
+        def copy(self, src, dst, target):
+            return pltpu.make_async_remote_copy(
+                src_ref=src, dst_ref=dst, send_sem=ssem, recv_sem=rsem.at[self.k],
+                device_id=target, device_id_type=MESH_ID,
+            )
+
+        def send(self, src, dst, target):
+            bytes_sent[0] += math.prod(src.shape) * 4
+            self.copy(src, dst, target).start()
+
+        def wait(self):
+            self.copy(self.like, self.like, {"batch": 1 - c}).wait_recv()
+
+    def one(src, dst, target):
+        group = Group(dst)
+        group.send(src, dst, target)
+        return group
+
+    def slot(place, j):
+        return lax.rem(place - j + 7, N)
 
     def at_peer(axis, d):
         return lax.rem(place[axis] + d, N)
@@ -148,29 +162,29 @@
         sqk[p, 0:32] = qt[32 * p : 32 * p + 32]
         sqk[p, 32:64] = kt[32 * p : 32 * p + 32]
     pl.semaphore_wait(barrier, greeted)
-    qk_in = []
+    qk_in = Group(rqk.at[pl.ds(0, 3)])
     for dy in (1, 3, 2):
         p = at_peer("seq_2", dy)
-        qk_in.append(send(sqk.at[p], rqk.at[y], {"seq_2": p}))
-    rqk[y] = sqk[y]
-    v_in = []
+        qk_in.send(sqk.at[p], rqk.at[dy - 1], {"seq_2": p})
+    rqk[3] = sqk[y]
+    v_in = Group(rv.at[pl.ds(0, 3)])
     for k, dy in enumerate(ORDER):
         p = at_peer("seq_2", dy)
         loads[("wv", k)].wait()
         v = mm(xb[...], wv[k]).astype(bf16).astype(f32)
         if dy:
             sv[k] = v
-            v_in.append(send(sv.at[k], rv.at[y], {"seq_2": p}))
+            v_in.send(sv.at[k], rv.at[dy - 1], {"seq_2": p})
         else:
-            rv[y] = v
+            rv[3] = v
     loads["u"].wait()
     for p in range(N):
         us[p] = ub[:, 256 * p : 256 * p + 256].astype(f32)
-    u_in = []
+    u_in = Group(ur.at[pl.ds(0, 3)])
     for dy in (1, 3, 2):
         p = at_peer("seq_2", dy)
-        u_in.append(send(us.at[p], ur.at[y], {"seq_2": p}))
-    ur[y] = us[y]
+        u_in.send(us.at[p], ur.at[dy - 1], {"seq_2": p})
+    ur[3] = us[y]
 
     for b in range(16):
         block = xb[:, 128 * b : 128 * b + 128].astype(f32).T
@@ -179,48 +193,45 @@
             xt2[i % 2, b // 4, row : row + 16] = block[16 * i : 16 * i + 16]
     chunk = [lax.rem(z + i + 1, N) for i in range(N)]
     after, before = at_peer("seq_2", 1), at_peer("seq_2", 3)
-    x_in = [[] for _ in range(N)]
+    x_in = [Group(xg.at[i, pl.ds(0, 5)]) for i in range(N)]
     passing = [None] * N
 
     def x_start(i):
         part = chunk[i]
-        mine = xg.at[part, y, c]
-        x_in[i].append(send(xt2.at[1 - c, part], mine, {"batch": 1 - c}))
-        same, cross = [], []
-        for p in (after, before):
-            same.append(send(xt2.at[c, part], mine, {"seq_2": p, "batch": c}))
-            cross.append(send(xt2.at[1 - c, part], mine, {"seq_2": p, "batch": 1 - c}))
-        xg[part, y, c] = xt2[c, part]
-        x_in[i] += [same[1], cross[0]]
-        passing[i] = (same[0], cross[1])
+        mine = xg.at[part, 2 * y + c]
+        x_in[i].send(xt2.at[1 - c, part], mine, {"batch": 1 - c})
+        up = one(xt2.at[c, part], mine, {"seq_2": after, "batch": c})
+        x_in[i].send(xt2.at[c, part], mine, {"seq_2": before, "batch": c})
+        x_in[i].send(xt2.at[1 - c, part], mine, {"seq_2": after, "batch": 1 - c})
+        down = one(xt2.at[1 - c, part], mine, {"seq_2": before, "batch": 1 - c})
+        xg[part, 2 * y + c] = xt2[c, part]
+        passing[i] = (up, down)
 
     def x_pass(i):
         part = chunk[i]
         up, down = passing[i]
-        up.wait_recv()
-        move = xg.at[part, before, c]
-        x_in[i].append(send(move, move, {"seq_2": after}))
-        down.wait_recv()
-        move = xg.at[part, after, 1 - c]
-        x_in[i].append(send(move, move, {"seq_2": before}))
+        up.wait()
+        move = xg.at[part, 2 * before + c]
+        x_in[i].send(move, move, {"seq_2": after})
+        down.wait()
+        move = xg.at[part, 2 * after + 1 - c]
+        x_in[i].send(move, move, {"seq_2": before})
 
     for i in range(N - 1):
         x_start(i)
 
-    for copy in qk_in:
-        copy.wait_recv()
+    qk_in.wait()
     for h in range(2):
         lo = 16 * h
-        uq = jnp.concatenate([rqk[j, lo : lo + 16] for j in range(N)], 1) * 0.5
-        uk = jnp.concatenate([rqk[j, 32 + lo : 48 + lo] for j in range(N)], 1) * 0.5
+        uq = jnp.concatenate([rqk[slot(y, j), lo : lo + 16] for j in range(N)], 1) * 0.5
+        uk = jnp.concatenate([rqk[slot(y, j), 32 + lo : 48 + lo] for j in range(N)], 1) * 0.5
         fq[h] = features(uq)
         fk[h] = features(uk)
-    for copy in v_in:
-        copy.wait_recv()
+    v_in.wait()
     ones = jnp.ones((16, TOK), bf16)
     for h in range(2):
         for j in range(N):
-            vb[h, 128 * j : 128 * j + 128] = rv[j, :, 128 * h : 128 * h + 128].astype(bf16)
+            vb[h, 128 * j : 128 * j + 128] = rv[slot(y, j), :, 128 * h : 128 * h + 128].astype(bf16)
 
     def put_state(st, h, state, norm):
         st[2 * h] = state[:80]
@@ -229,43 +240,44 @@
         st[2 * h + 1, 74:75] = jnp.concatenate([norm[:, 128:], jnp.zeros((1, 96), f32)], 1)
 
     def get_state(pf, h):
-        state = jnp.concatenate([pf[2 * h], pf[2 * h + 1]], 0)
-        norm = jnp.concatenate([pf[2 * h + 1, 73:74], pf[2 * h + 1, 74:75, :32]], 1)
+        low, high = slot(x, 2 * h), slot(x, 2 * h + 1)
+        state = jnp.concatenate([pf[low], pf[high]], 0)
+        norm = jnp.concatenate([pf[high, 73:74], pf[high, 74:75, :32]], 1)
         return state, norm
 
     for h in range(2):
         put_state(st1, h, mm(fk[h], vb[h]), mm_nt(ones, fk[h])[:1])
 
     def scan_start(st, xr):
-        copies = []
+        group = Group(xr.at[pl.ds(0, 3)])
         for d in (1, 3, 2):
             p = at_peer("seq_1", d)
-            copies.append(send(st.at[p], xr.at[x], {"seq_1": p}))
-        xr[x] = st[x]
-        return copies
-
-    def scan_mid(copies, xr, zs, zr):
-        for copy in copies:
-            copy.wait_recv()
+            group.send(st.at[p], xr.at[d - 1], {"seq_1": p})
+        xr[3] = st[x]
+        return group
+
+    def scan_mid(group, xr, zs, zr):
+        group.wait()
         zs[...] = (xr[0] + xr[1]) + (xr[2] + xr[3])
-        return [send(zs, zr.at[z], {"seq_0": at_peer("seq_0", d)}) for d in (1, 3, 2)]
-
-    def scan_back(copies, xr, zr, pb, pf, later):
-        for copy in copies:
-            copy.wait_recv()
+        group = Group(zr)
+        for d in (1, 3, 2):
+            group.send(zs, zr.at[d - 1], {"seq_0": at_peer("seq_0", d)})
+        return group
+
+    def scan_back(group, xr, zr, pb, pf, later):
+        group.wait()
         run = jnp.zeros((80, 128), f32)
         for d in (1, 2, 3):
-            p = at_peer("seq_0", d)
-            run = run + jnp.where(p > z if later else p < z, zr[p], 0.0)
+            run = run + jnp.where(z < d if later else z >= d, zr[d - 1], 0.0)
         for i in reversed(range(N)) if later else range(N):
             pb[i] = run
-            run = run + xr[i]
-        out = []
+            run = run + xr[slot(x, i)]
+        group = Group(pf.at[pl.ds(0, 3)])
         for d in (1, 3, 2):
             p = at_peer("seq_1", d)
-            out.append(send(pb.at[p], pf.at[x], {"seq_1": p}))
-        pf[x] = pb[x]
-        return out
+            group.send(pb.at[p], pf.at[d - 1], {"seq_1": p})
+        pf[3] = pb[x]
+        return group
 
     keep = lax.broadcasted_iota(jnp.int32, (TOK, TOK), 1) >= lax.broadcasted_iota(
         jnp.int32, (TOK, TOK), 0
@@ -274,7 +286,7 @@
     def local_forward(h):
         for j in range(N):
             vt[h, :, 128 * j : 128 * j + 128] = (
-                rv[j, :, 128 * h : 128 * h + 128].T.astype(bf16)
+                rv[slot(y, j), :, 128 * h : 128 * h + 128].T.astype(bf16)
             )
         scores = jnp.where(keep, mm_tn(fk[h], fq[h]), 0.0)
         dloc[h] = jnp.broadcast_to(jnp.sum(scores, 0, keepdims=True), (8, TOK))
@@ -286,13 +298,11 @@
     move = scan_mid(move, xr1, zs1, zr1)
     local_forward(1)
     move = scan_back(move, xr1, zr1, pb1, pf1, False)
-    for copy in u_in:
-        copy.wait_recv()
+    u_in.wait()
     for h in range(2):
         for j in range(N):
-            ut[h, :, 128 * j : 128 * j + 128] = ur[j, :, 128 * h : 128 * h + 128].T
-    for copy in move:
-        copy.wait_recv()
+            ut[h, :, 128 * j : 128 * j + 128] = ur[slot(y, j), :, 128 * h : 128 * h + 128].T
+    move.wait()
 
     for h in range(2):
         state, norm = get_state(pf1, h)
@@ -337,10 +347,9 @@
     move = scan_back(move, xr2, zr2, pb2, pf2, True)
     for h in range(2):
         lo = 16 * h
-        uq = jnp.concatenate([rqk[j, lo : lo + 16] for j in range(N)], 1) * 0.5
+        uq = jnp.concatenate([rqk[slot(y, j), lo : lo + 16] for j in range(N)], 1) * 0.5
         put_grad(h, 256, uq, gfq[h])
-    for copy in move:
-        copy.wait_recv()
+    move.wait()
     first16 = lax.broadcasted_iota(jnp.int32, (16, TOK), 0) < 2
     flag = jnp.where(first16, 1.0, 0.0).astype(bf16)
     for h in range(2):
@@ -353,22 +362,44 @@
             gg[c, j, 128 * h : 128 * h + 128] = g_val[:, 128 * j : 128 * j + 128]
         g_fk = gfk[h] + mm(backb, vt[h]) + mm_tn(rows16(b_hi, b_lo), flag)
         lo = 32 + 16 * h
-        uk = jnp.concatenate([rqk[j, lo : lo + 16] for j in range(N)], 1) * 0.5
+        uk = jnp.concatenate([rqk[slot(y, j), lo : lo + 16] for j in range(N)], 1) * 0.5
         put_grad(h, 288, uk, g_fk)
 
-    pair_g = send(gg.at[c], gg.at[c], {"batch": 1 - c})
+    pair_g = one(gg.at[c], gg.at[c], {"batch": 1 - c})
     x_pass(2)
-    pair_g.wait_recv()
+    def gin_add(k, fresh):
+        g_v = gb[(3 - ORDER[k]) % 4, 0:256].T.astype(bf16)
+
+        def columns(i, carry):
+            rows = pl.ds(pl.multiple_of(i * 512, 512), 512)
+            part = mm_nt(g_v, wv[k, rows])
+            gacc[:, rows] = part if fresh else gacc[:, rows] + part
+            return carry
+
+        lax.fori_loop(0, N, columns, 0)
+
+    gb[3] = gg[c, y]
+    gin_add(3, True)
+    x_pass(3)
+    g_thin = Group(gb.at[pl.ds(0, 3), pl.ds(256, 64)])
+    g_wide = {}
+    for dy in (2, 1, 3):
+        p = at_peer("seq_2", dy)
+        g_thin.send(gg.at[c, p, pl.ds(256, 64)], gb.at[dy - 1, pl.ds(256, 64)], {"seq_2": p})
+    for dy in (2, 1, 3):
+        p = at_peer("seq_2", dy)
+        g_wide[dy] = one(gg.at[c, p, pl.ds(0, 256)], gb.at[dy - 1, pl.ds(0, 256)], {"seq_2": p})
+    pair_g.wait()
     rhs = jnp.concatenate([gg[i, j].astype(bf16) for j in range(N) for i in range(2)], 1)
 
-    a_in, b_in = [], []
+    a_in = [Group(ra.at[i]) for i in range(N)]
+    b_in = Group(rb)
 
     def weights_of(i):
         part = chunk[i]
-        for copy in x_in[i]:
-            copy.wait_recv()
+        x_in[i].wait()
         lhs = jnp.concatenate(
-            [xg[part, j, k].astype(bf16) for j in range(N) for k in range(2)], 1
+            [xg[part, j].astype(bf16) for j in range(8)], 1
         )
         out = mm_nt(lhs, rhs)
         for xx in range(N):
@@ -378,18 +409,16 @@
                 da[i, xx, 24 * j : 24 * j + 16] = own[:, :128]
                 da[i, xx, 24 * j + 16 : 24 * j + 24] = jnp.concatenate([thin[:8], thin[8:]], 1)
                 db[i, xx, 16 * j : 16 * j + 16] = own[:, 128:256]
-        a_in.append([])
         for k, d in enumerate((1, 3, 2)):
             p = at_peer("seq_1", d)
-            a_in[i].append(send(da.at[i, p], ra.at[i, k], {"seq_1": p}))
+            a_in[i].send(da.at[i, p], ra.at[i, k], {"seq_1": p})
         if i < N - 1:
-            b_in.append(send(db.at[i], rb.at[i], {"seq_0": part}))
-
-    last = []
+            b_in.send(db.at[i], rb.at[i], {"seq_0": part})
+
+    a_last, b_last = Group(fa.at[pl.ds(0, 15)]), Group(fb.at[pl.ds(0, 15)])
 
     def a_onward(i):
-        for copy in a_in[i]:
-            copy.wait_recv()
+        a_in[i].wait()
         total = (da[i, x] + ra[i, 0]) + (ra[i, 1] + ra[i, 2])
         for j in range(N):
             sa[i, j] = total[24 * j : 24 * j + 24]
@@ -399,25 +428,16 @@
             if i < N - 1:
                 target["seq_0"] = chunk[i]
             elif dy == 0:
-                fa[i, y] = sa[i, y]
+                fa[15] = sa[i, y]
                 continue
-            last.append(send(sa.at[i, p], fa.at[i, y], target))
+            a_last.send(sa.at[i, p], fa.at[4 * i + (dy + 3) % 4], target)
 
     weights_of(0)
     weights_of(1)
     a_onward(0)
     weights_of(2)
-    x_pass(3)
-    g_in = []
-    for dy in (1, 3, 2):
-        p = at_peer("seq_2", dy)
-        g_in.append(send(gg.at[c, p], gb.at[y], {"seq_2": p}))
-    gb[y] = gg[c, y]
-    a_onward(1)
-    a_onward(2)
     weights_of(3)
-    for copy in b_in:
-        copy.wait_recv()
+    b_in.wait()
     for xx in range(N):
         db[3, xx] = (db[3, xx] + rb[0, xx]) + (rb[1, xx] + rb[2, xx])
     for d in ORDER:
@@ -426,46 +446,64 @@
             p = at_peer("seq_2", dy)
             piece = db.at[3, px, pl.ds(pl.multiple_of(p * 16, 16), 16)]
             if d or dy:
-                last.append(send(piece, fb.at[d, y], {"seq_1": px, "seq_2": p}))
+                into = fb.at[4 * ((d + 3) % 4) + (dy + 3) % 4]
+                b_last.send(piece, into, {"seq_1": px, "seq_2": p})
             else:
-                fb[0, y] = piece[...]
+                fb[15] = piece[...]
+    a_onward(1)
+    a_onward(2)
+
+    g_thin.wait()
+    g_q = jnp.concatenate([gb[slot(y, j), 256:288] for j in range(N)], 0).T.astype(bf16)
+    g_k = jnp.concatenate([gb[slot(y, j), 288:320] for j in range(N)], 0).T.astype(bf16)
+
+    def thin_columns(i, carry):
+        rows = pl.ds(pl.multiple_of(i * 512, 512), 512)
+        gacc[:, rows] = gacc[:, rows] + (mm_nt(g_q, wq[rows]) + mm_nt(g_k, wk[rows]))
+        return carry
+
+    lax.fori_loop(0, N, thin_columns, 0)
     a_onward(3)
-
-    for copy in g_in:
-        copy.wait_recv()
-    g_q = jnp.concatenate([gb[j, 256:288] for j in range(N)], 0).T.astype(bf16)
-    g_k = jnp.concatenate([gb[j, 288:320] for j in range(N)], 0).T.astype(bf16)
-    g_v = []
-    for k, dy in enumerate(ORDER):
-        p = at_peer("seq_2", dy)
-        g_v.append(gb[p, 0:256].T.astype(bf16))
+    g_wide[1].wait()
+    gin_add(1, False)
+    g_wide[3].wait()
+    gin_add(0, False)
+    g_wide[2].wait()
+    g_v = gb[1, 0:256].T.astype(bf16)
 
     def inputs_of(i, carry):
         rows = pl.ds(pl.multiple_of(i * 512, 512), 512)
-        acc = mm_nt(g_q, wq[rows]) + mm_nt(g_k, wk[rows])
-        for k in range(N):
-            acc = acc + mm_nt(g_v[k], wv[k, rows])
-        gi[:, rows] = acc.astype(bf16)
+        gi[:, rows] = (gacc[:, rows] + mm_nt(g_v, wv[2, rows])).astype(bf16)
         return carry
 
     lax.fori_loop(0, N, inputs_of, 0)
     out_copy = pltpu.make_async_copy(gi, gin.at[0], osem)
     out_copy.start()
-    for copy in last:
-        copy.wait_recv()
-    for p in range(N):
-        both = (fa[0, p] + fa[1, p]) + (fa[2, p] + fa[3, p])
-        res[p, 0:16] = both[:16]
-        res[p, 16:32] = (fb[0, p] + fb[1, p]) + (fb[2, p] + fb[3, p])
-        res[p, 32:40] = both[16:]
+    a_last.wait()
+    b_last.wait()
+    for dy in range(N):
+        p = at_peer("seq_2", (4 - dy) % 4)
+        k = (dy + 3) % 4
+        both = (fa[k] + fa[4 + k]) + (fa[8 + k] + fa[12 + k])
+        rs[p, 0:16] = both[:16]
+        rs[p, 16:32] = (fb[k] + fb[4 + k]) + (fb[8 + k] + fb[12 + k])
+        rs[p, 32:40] = both[16:]
+    res_copy = pltpu.make_async_copy(rs, res, rsm)
+    res_copy.start()
     out_copy.wait()
-    assert used[0] == SENDS
-    for copy in started:
-        copy.wait_send()
-
-
-def finish(gin_ref, res_ref, gin_out, gwq, gwk, gwv):
-    gin_out[...] = gin_ref[...]
+    res_copy.wait()
+    assert groups[0] == GROUPS and bytes_sent[0] == SENT * 512
+    group = Group(None)
+    group.k = 0
+    group.copy(total, total, {"batch": 1 - c}).wait_send()
+
+
+def finish(gin_ref, res_hbm, gin_out, gwq, gwk, gwv, res_ref, sems):
+    copy = pltpu.make_async_copy(gin_ref, gin_out, sems.at[0])
+    copy.start()
+    fetch = pltpu.make_async_copy(res_hbm, res_ref, sems.at[1])
+    fetch.start()
+    fetch.wait()
     lane = lax.broadcasted_iota(jnp.int32, (16, 128), 1) // 32
     w_q = jnp.zeros((16, 128), f32)
     w_k = jnp.zeros((16, 128), f32)
@@ -480,9 +518,14 @@
         w_k = jnp.where(lane == p, from_k, w_k)
     gwq[...] = w_q
     gwk[...] = w_k
-
-
-SENDS = 3 + 3 + 3 + 18 + 1 + 4 * 7 + 3 + 12 + 3 + 15 + 15
+    copy.wait()
+
+
+GROUPS = 3 + 6 + 4 * 3 + 1 + 4 + 4 + 1 + 2
+SENT = (
+    3 * 64 + 6 * 256 + 18 * 80 + 28 * 256 + 4 * 320 + 3 * 320
+    + 12 * 96 + 12 * 64 + 15 * 24 + 15 * 16
+)
 
 
 def body(inputs, cotangent, w_query, w_key, w_value):
@@ -491,11 +534,11 @@
     here = pl.BlockSpec(memory_space=pltpu.VMEM)
     scan = [
         vmem((4, 80, 128), f32), vmem((4, 80, 128), f32), vmem((80, 128), f32),
-        vmem((4, 80, 128), f32), vmem((4, 80, 128), f32), vmem((4, 80, 128), f32),
+        vmem((3, 80, 128), f32), vmem((4, 80, 128), f32), vmem((4, 80, 128), f32),
     ]
     scratch = [
         vmem((BLK, D), bf16), vmem((BLK, 1024), bf16), vmem((D, 128), bf16), vmem((D, 128), bf16),
-        vmem((4, D, 256), bf16), vmem((2, 4, 256, 128), f32), vmem((4, 4, 2, 256, 128), f32),
+        vmem((4, D, 256), bf16), vmem((2, 4, 256, 128), f32), vmem((4, 8, 256, 128), f32),
         vmem((4, 64, 128), f32), vmem((3, 128, 256), f32), vmem((4, 64, 128), f32),
         vmem((4, 128, 256), f32), vmem((4, 128, 256), f32), vmem((4, 128, 256), f32),
         vmem((2, FP, TOK), bf16), vmem((2, FP, TOK), bf16), vmem((2, TOK, 128), bf16),
@@ -505,20 +548,21 @@
         vmem((2, 128, TOK), f32), vmem((2, FP, 128), bf16), vmem((2, 8, FP), f32),
         *scan, *scan,
         vmem((2, 4, 320, 128), f32), vmem((4, 320, 128), f32), vmem((BLK, D), bf16),
-        vmem((4, 4, 96, 128), f32), vmem((4, 4, 64, 128), f32),
+        vmem((BLK, D), f32), vmem((4, 4, 96, 128), f32), vmem((4, 4, 64, 128), f32),
         vmem((4, 3, 96, 128), f32), vmem((3, 4, 64, 128), f32),
-        vmem((4, 4, 24, 128), f32), vmem((4, 4, 24, 128), f32), vmem((4, 4, 16, 128), f32),
-        pltpu.SemaphoreType.DMA((8,)), pltpu.SemaphoreType.DMA, pltpu.SemaphoreType.DMA((SENDS,)),
-        pltpu.SemaphoreType.DMA((SENDS,)),
+        vmem((4, 4, 24, 128), f32), vmem((16, 24, 128), f32), vmem((16, 16, 128), f32),
+        vmem((4, 40, 128), f32), vmem((SENT, 128), f32),
+        pltpu.SemaphoreType.DMA((8,)), pltpu.SemaphoreType.DMA, pltpu.SemaphoreType.DMA, pltpu.SemaphoreType.DMA,
+        pltpu.SemaphoreType.DMA((GROUPS,)),
     ]
     gin, res = pl.pallas_call(
         kernel,
         out_shape=(
-            jax.ShapeDtypeStruct((1, BLK, D), bf16),
-            jax.ShapeDtypeStruct((4, 40, 128), f32),
+            pltpu.VMEM((1, BLK, D), bf16),
+            pltpu.VMEM((4, 40, 128), f32),
         ),
-        in_specs=[hbm] * 5,
-        out_specs=(hbm, here),
+        in_specs=[pl.BlockSpec(memory_space=pltpu.HBM)] * 5,
+        out_specs=(hbm, hbm),
         scratch_shapes=scratch,
         compiler_params=pltpu.CompilerParams(
             collective_id=0, has_side_effects=True, vmem_limit_bytes=60 * 1024 * 1024
@@ -532,8 +576,10 @@
             jax.ShapeDtypeStruct((16, 128), f32),
             jax.ShapeDtypeStruct((16, 1024), f32),
         ),
-        in_specs=[here] * 2,
-        out_specs=(here,) * 4,
+        in_specs=[hbm] * 2,
+        out_specs=(pl.BlockSpec(memory_space=pltpu.HBM), here, here, here),
+        scratch_shapes=[pltpu.VMEM((4, 40, 128), f32), pltpu.SemaphoreType.DMA((2,))],
+        compiler_params=pltpu.CompilerParams(vmem_limit_bytes=4 * 1024 * 1024),
     )(gin, res)
 
 

time: 75.8 us -> 70.2 us (0.926)
  Pallas kernels: 75 us -> 69.4 us
    pallas_call x1, Pallas kernels: 73.1 us -> 68 us  [body(): pl.pallas_call(kernel, out_shape=(pltpu.VMEM((1, BLK, D), bf16), pltpu.VM...]
where the time goes in v3:
time: 70.2 us; the launch traced here: 70.1 us
  Pallas kernels  69.4 us (99%)
    pallas_call x1, Pallas kernels, body(): pl.pallas_call(kernel, out_shape=(pltpu.VMEM((1, BLK, D), bf16), pltpu.VM...  68 us
    pallas_call x1, Pallas kernels, body(): pl.pallas_call(finish, out_shape=(jax.ShapeDtypeStruct((1, BLK, D), bf16)...  1.45 us

profile of v3, /device:TPU:0, one launch (start us, length us, event | category | flops | bytes accessed | tf_op | source)
XLA Modules:
  0.0 70.1 jit_solution(5027866882929600774)
XLA Ops:
  0.6 68.0 %shard_map.84 = (bf16[1,128,2048]{2,1,0:T(8,128)(2,1)S(1)}, f32[4,40,128]{2,1,0:T(8,128)S(1)}) custom-call(bf16[1,128,2048]{2,1,0:T(8,128)(2,1)} %x_hbm.1, bf16[1,128,1024]{2,1,0:T(8,128)(2,1)} %u_hbm.1, bf16[2048,128]{1,0:T(8,128)(2,1)} %wq_hbm.1, bf16[2048,128]{1,0:T(8,128)(2,1)} %wk_hbm.1, bf16[2048,1024]{1,0:T(8,128)(2,1)} %wv_hbm.1), custom_call_target="tpu_custom_call" | custom-call | tf_op jit(solution)/shard_map/pallas_call | solution.py:558
  68.6 1.4 %shard_map.85 = (bf16[1,128,2048]{2,1,0:T(8,128)(2,1)}, f32[16,128]{1,0:T(8,128)}, f32[16,128]{1,0:T(8,128)}, f32[16,1024]{1,0:T(8,128)}) custom-call(bf16[1,128,2048]{2,1,0:T(8,128)(2,1)S(1)} %get-tuple-element.6.gin_ref, f32[4,40,128]{2,1,0:T(8,128)S(1)} %get-tuple-element.7.res_hbm), custom_call_target="tpu_custom_call" | custom-call | tf_op jit(solution)/shard_map/pallas_call | solution.py:571

commit v4 on v3

--- a/solution.py
+++ b/solution.py
@@ -78,14 +78,14 @@
 
 def kernel(
     x_hbm, u_hbm, wq_hbm, wk_hbm, wv_hbm,
-    gin, res,
+    gin, gwq, gwk, gwv,
     xb, ub, wq, wk, wv, xt2, xg,
     sqk, sv, rqk, rv, us, ur,
     fq, fk, vb, vt, ut, at, num, dloc, gnb, gdr, gfq, gfk, gvt, stb, nrm,
     st1, xr1, zs1, zr1, pb1, pf1,
     st2, xr2, zs2, zr2, pb2, pf2,
-    gg, gb, gi, gacc, da, db, ra, rb, sa, fa, fb, rs, total,
-    lsem, osem, rsm, ssem, rsem,
+    gg, gb, gi, gacc, da, db, ra, rb, sa, fa, fb, fc, yb, yr, rs, rs_q, rs_k, rs_v, total,
+    lsem, osem, ssem, rsem,
 ):
     z, x, y, c = (lax.axis_index(a) for a in SEQ_BATCH)
     place = {"seq_0": z, "seq_1": x, "seq_2": y}
@@ -96,15 +96,15 @@
             self.like, self.k = like, groups[0]
             groups[0] += 1
 
-        def copy(self, src, dst, target):
+        def copy(self, src, dst, target, k=0):
             return pltpu.make_async_remote_copy(
-                src_ref=src, dst_ref=dst, send_sem=ssem, recv_sem=rsem.at[self.k],
+                src_ref=src, dst_ref=dst, send_sem=ssem.at[k], recv_sem=rsem.at[self.k],
                 device_id=target, device_id_type=MESH_ID,
             )
 
-        def send(self, src, dst, target):
-            bytes_sent[0] += math.prod(src.shape) * 4
-            self.copy(src, dst, target).start()
+        def send(self, src, dst, target, k=0):
+            bytes_sent[0] += math.prod(src.shape) * 4 if k == 0 else 0
+            self.copy(src, dst, target, k).start()
 
         def wait(self):
             self.copy(self.like, self.like, {"batch": 1 - c}).wait_recv()
@@ -138,15 +138,17 @@
     greeted = 0
     for d in range(N):
         for e in range(N):
-            pairs = [("seq_0", "seq_2")] if d or e else []
-            if d:
-                pairs.append(("seq_1", "seq_2"))
-            for first, second in pairs:
+            if d or e:
                 greeted += 1
                 pl.semaphore_signal(
                     barrier, inc=1, device_id_type=MESH_ID,
-                    device_id={first: at_peer(first, d), second: at_peer(second, e)},
+                    device_id={"seq_0": at_peer("seq_0", d), "seq_1": at_peer("seq_1", e)},
                 )
+        if d:
+            greeted += 1
+            pl.semaphore_signal(
+                barrier, inc=1, device_id_type=MESH_ID, device_id={"seq_2": at_peer("seq_2", d)}
+            )
         greeted += 1
         pl.semaphore_signal(
             barrier, inc=1, device_id_type=MESH_ID,
@@ -193,7 +195,7 @@
             xt2[i % 2, b // 4, row : row + 16] = block[16 * i : 16 * i + 16]
     chunk = [lax.rem(z + i + 1, N) for i in range(N)]
     after, before = at_peer("seq_2", 1), at_peer("seq_2", 3)
-    x_in = [Group(xg.at[i, pl.ds(0, 5)]) for i in range(N)]
+    x_in = [Group(xg.at[i, pl.ds(0, 5 if i < 3 else 4)]) for i in range(N)]
     passing = [None] * N
 
     def x_start(i):
@@ -206,6 +208,26 @@
         down = one(xt2.at[1 - c, part], mine, {"seq_2": before, "batch": 1 - c})
         xg[part, 2 * y + c] = xt2[c, part]
         passing[i] = (up, down)
+
+    to_pair = one(xt2.at[1 - c, chunk[3]], xg.at[chunk[3], 2 * y + c], {"batch": 1 - c})
+    xg[chunk[3], 2 * y + c] = xt2[c, chunk[3]]
+
+    def x_start_last():
+        part = chunk[3]
+        mine = xg.at[part, 2 * y + c]
+        up, down = Group(xg.at[3, 0]), Group(xg.at[3, 0])
+        passing[3] = (up, down)
+        up.send(xt2.at[c, part], mine, {"seq_2": after})
+        x_in[3].send(xt2.at[c, part], mine, {"seq_2": before})
+        to_pair.wait()
+
+        @pl.when(c == 1)
+        def _():
+            for e in range(2):
+                src = xg.at[part, 2 * y] if e else xt2.at[0, part]
+                into = xg.at[part, 2 * y + 1 - e]
+                x_in[3].send(src, into, {"seq_2": after, "batch": e}, 1)
+                down.send(src, into, {"seq_2": before, "batch": e}, 1)
 
     def x_pass(i):
         part = chunk[i]
@@ -339,7 +361,7 @@
 
     move = scan_start(st2, xr2)
     x_pass(0)
-    x_start(3)
+    x_start_last()
     local_backward(0)
     move = scan_mid(move, xr2, zs2, zr2)
     x_pass(1)
@@ -367,37 +389,17 @@
 
     pair_g = one(gg.at[c], gg.at[c], {"batch": 1 - c})
     x_pass(2)
-    def gin_add(k, fresh):
-        g_v = gb[(3 - ORDER[k]) % 4, 0:256].T.astype(bf16)
-
-        def columns(i, carry):
-            rows = pl.ds(pl.multiple_of(i * 512, 512), 512)
-            part = mm_nt(g_v, wv[k, rows])
-            gacc[:, rows] = part if fresh else gacc[:, rows] + part
-            return carry
-
-        lax.fori_loop(0, N, columns, 0)
-
     gb[3] = gg[c, y]
-    gin_add(3, True)
+    gacc[...] = mm(wv[3], gb[3, 0:256].astype(bf16))
     x_pass(3)
-    g_thin = Group(gb.at[pl.ds(0, 3), pl.ds(256, 64)])
-    g_wide = {}
-    for dy in (2, 1, 3):
-        p = at_peer("seq_2", dy)
-        g_thin.send(gg.at[c, p, pl.ds(256, 64)], gb.at[dy - 1, pl.ds(256, 64)], {"seq_2": p})
-    for dy in (2, 1, 3):
-        p = at_peer("seq_2", dy)
-        g_wide[dy] = one(gg.at[c, p, pl.ds(0, 256)], gb.at[dy - 1, pl.ds(0, 256)], {"seq_2": p})
     pair_g.wait()
     rhs = jnp.concatenate([gg[i, j].astype(bf16) for j in range(N) for i in range(2)], 1)
 
     a_in = [Group(ra.at[i]) for i in range(N)]
-    b_in = Group(rb)
+    b_in, c_last = Group(rb), Group(fc)
 
     def weights_of(i):
         part = chunk[i]
-        x_in[i].wait()
         lhs = jnp.concatenate(
             [xg[part, j].astype(bf16) for j in range(8)], 1
         )
@@ -412,126 +414,129 @@
         for k, d in enumerate((1, 3, 2)):
             p = at_peer("seq_1", d)
             a_in[i].send(da.at[i, p], ra.at[i, k], {"seq_1": p})
-        if i < N - 1:
+        if i < 2:
             b_in.send(db.at[i], rb.at[i], {"seq_0": part})
-
-    a_last, b_last = Group(fa.at[pl.ds(0, 15)]), Group(fb.at[pl.ds(0, 15)])
+        elif i == 2:
+            for d in (1, 3, 2, 0):
+                p = at_peer("seq_1", d)
+                c_last.send(db.at[i, p], fc.at[(d + 3) % 4], {"seq_0": part, "seq_1": p})
+
+    a_last, b_last = Group(fa), Group(fb)
 
     def a_onward(i):
         a_in[i].wait()
-        total = (da[i, x] + ra[i, 0]) + (ra[i, 1] + ra[i, 2])
-        for j in range(N):
-            sa[i, j] = total[24 * j : 24 * j + 24]
-        for dy in ORDER:
-            p = at_peer("seq_2", dy)
-            target = {"seq_2": p}
-            if i < N - 1:
-                target["seq_0"] = chunk[i]
-            elif dy == 0:
-                fa[15] = sa[i, y]
-                continue
-            a_last.send(sa.at[i, p], fa.at[4 * i + (dy + 3) % 4], target)
-
+        sa[i] = (da[i, x] + ra[i, 0]) + (ra[i, 1] + ra[i, 2])
+        if i < N - 1:
+            a_last.send(sa.at[i], fa.at[i], {"seq_0": chunk[i]})
+
+    x_in[0].wait()
     weights_of(0)
+    x_in[1].wait()
     weights_of(1)
+    x_in[2].wait()
+    weights_of(2)
+    g_thin = Group(gb.at[pl.ds(0, 3), pl.ds(256, 64)])
     a_onward(0)
-    weights_of(2)
+    x_in[3].wait()
+    g_wide = {}
+    for dy in (2, 1, 3):
+        p = at_peer("seq_2", dy)
+        g_thin.send(gg.at[c, p, pl.ds(256, 64)], gb.at[dy - 1, pl.ds(256, 64)], {"seq_2": p})
+    for dy in (2, 1, 3):
+        p = at_peer("seq_2", dy)
+        g_wide[dy] = one(gg.at[c, p, pl.ds(0, 256)], gb.at[dy - 1, pl.ds(0, 256)], {"seq_2": p})
     weights_of(3)
     b_in.wait()
     for xx in range(N):
-        db[3, xx] = (db[3, xx] + rb[0, xx]) + (rb[1, xx] + rb[2, xx])
-    for d in ORDER:
-        px = at_peer("seq_1", d)
-        for dy in ORDER:
-            p = at_peer("seq_2", dy)
-            piece = db.at[3, px, pl.ds(pl.multiple_of(p * 16, 16), 16)]
-            if d or dy:
-                into = fb.at[4 * ((d + 3) % 4) + (dy + 3) % 4]
-                b_last.send(piece, into, {"seq_1": px, "seq_2": p})
-            else:
-                fb[15] = piece[...]
+        db[3, xx] = db[3, xx] + (rb[0, xx] + rb[1, xx])
+    for d in (1, 3, 2):
+        p = at_peer("seq_1", d)
+        b_last.send(db.at[3, p], fb.at[d - 1], {"seq_1": p})
     a_onward(1)
     a_onward(2)
 
-    g_thin.wait()
-    g_q = jnp.concatenate([gb[slot(y, j), 256:288] for j in range(N)], 0).T.astype(bf16)
-    g_k = jnp.concatenate([gb[slot(y, j), 288:320] for j in range(N)], 0).T.astype(bf16)
-
-    def thin_columns(i, carry):
-        rows = pl.ds(pl.multiple_of(i * 512, 512), 512)
-        gacc[:, rows] = gacc[:, rows] + (mm_nt(g_q, wq[rows]) + mm_nt(g_k, wk[rows]))
-        return carry
-
-    lax.fori_loop(0, N, thin_columns, 0)
     a_onward(3)
-    g_wide[1].wait()
-    gin_add(1, False)
-    g_wide[3].wait()
-    gin_add(0, False)
-    g_wide[2].wait()
-    g_v = gb[1, 0:256].T.astype(bf16)
-
-    def inputs_of(i, carry):
-        rows = pl.ds(pl.multiple_of(i * 512, 512), 512)
-        gi[:, rows] = (gacc[:, rows] + mm_nt(g_v, wv[2, rows])).astype(bf16)
-        return carry
-
-    lax.fori_loop(0, N, inputs_of, 0)
-    out_copy = pltpu.make_async_copy(gi, gin.at[0], osem)
-    out_copy.start()
     a_last.wait()
     b_last.wait()
+    c_last.wait()
+    sum_a = (sa[3] + fa[0]) + (fa[1] + fa[2])
+    sum_b = (db[3, x] + fb[0]) + (fb[1] + fb[2])
+    sum_b = sum_b + ((fc[0] + fc[1]) + (fc[2] + fc[3]))
+    for j in range(N):
+        yb[j, 0:24] = sum_a[24 * j : 24 * j + 24]
+        yb[j, 24:40] = sum_b[16 * j : 16 * j + 16]
+    y_in = Group(yr.at[pl.ds(0, 3)])
+    for dy in (2, 1, 3):
+        p = at_peer("seq_2", dy)
+        y_in.send(yb.at[p], yr.at[dy - 1], {"seq_2": p})
+    yr[3] = yb[y]
+    g_thin.wait()
+    g_wide[2].wait()
+    rows = [gb[slot(y, j), 256:288] for j in range(N)] + [gb[slot(y, j), 288:320] for j in range(N)]
+    part = jnp.concatenate(rows + [gb[1, 0:256]], 0).astype(bf16)
+    gacc[...] = gacc[...] + mm(jnp.concatenate([wq[...], wk[...], wv[2]], 1), part)
+    g_wide[1].wait()
+    g_wide[3].wait()
+    part = jnp.concatenate([gb[2, 0:256], gb[0, 0:256]], 0).astype(bf16)
+    gacc[...] = gacc[...] + mm(jnp.concatenate([wv[0], wv[1]], 1), part)
+    for i in range(16):
+        gi[:, 128 * i : 128 * i + 128] = gacc[128 * i : 128 * i + 128].T.astype(bf16)
+    out_copy = pltpu.make_async_copy(gi, gin.at[0], osem.at[0])
+    out_copy.start()
+    y_in.wait()
     for dy in range(N):
-        p = at_peer("seq_2", (4 - dy) % 4)
-        k = (dy + 3) % 4
-        both = (fa[k] + fa[4 + k]) + (fa[8 + k] + fa[12 + k])
-        rs[p, 0:16] = both[:16]
-        rs[p, 16:32] = (fb[k] + fb[4 + k]) + (fb[8 + k] + fb[12 + k])
-        rs[p, 32:40] = both[16:]
-    res_copy = pltpu.make_async_copy(rs, res, rsm)
-    res_copy.start()
-    out_copy.wait()
-    res_copy.wait()
-    assert groups[0] == GROUPS and bytes_sent[0] == SENT * 512
-    group = Group(None)
-    group.k = 0
-    group.copy(total, total, {"batch": 1 - c}).wait_send()
-
-
-def finish(gin_ref, res_hbm, gin_out, gwq, gwk, gwv, res_ref, sems):
-    copy = pltpu.make_async_copy(gin_ref, gin_out, sems.at[0])
-    copy.start()
-    fetch = pltpu.make_async_copy(res_hbm, res_ref, sems.at[1])
-    fetch.start()
-    fetch.wait()
+        rs[at_peer("seq_2", (4 - dy) % 4)] = yr[(dy + 3) % 4]
     lane = lax.broadcasted_iota(jnp.int32, (16, 128), 1) // 32
     w_q = jnp.zeros((16, 128), f32)
     w_k = jnp.zeros((16, 128), f32)
     for p in range(N):
-        gwv[:, 256 * p : 256 * p + 128] = res_ref[p, 0:16]
-        gwv[:, 256 * p + 128 : 256 * p + 256] = res_ref[p, 16:32]
-        thin = res_ref[p, 32:40]
+        rs_v[:, 256 * p : 256 * p + 128] = rs[p, 0:16]
+        rs_v[:, 256 * p + 128 : 256 * p + 256] = rs[p, 24:40]
+        thin = rs[p, 16:24]
         thin = jnp.concatenate([thin, pltpu.roll(thin, 64, 1)], 0)
         from_q = pltpu.roll(thin, 32 * p, 1) if p else thin
         w_q = jnp.where(lane == p, from_q, w_q)
         from_k = pltpu.roll(thin, (32 * p + 96) % 128, 1) if p != 1 else thin
         w_k = jnp.where(lane == p, from_k, w_k)
-    gwq[...] = w_q
-    gwk[...] = w_k
-    copy.wait()
-
-
-GROUPS = 3 + 6 + 4 * 3 + 1 + 4 + 4 + 1 + 2
+    rs_q[...] = w_q
+    rs_k[...] = w_k
+    results = [out_copy]
+    for i, (src, dst) in enumerate(((rs_q, gwq), (rs_k, gwk), (rs_v, gwv))):
+        results.append(pltpu.make_async_copy(src, dst, osem.at[i + 1]))
+        results[-1].start()
+    for copy in results:
+        copy.wait()
+    assert groups[0] == GROUPS and bytes_sent[0] == SENT * 512
+    to_pair.copy(total, total, {"batch": 1 - c}).wait_send()
+
+    @pl.when(c == 1)
+    def _():
+        many = total.at[pl.ds(0, 4 * 256)]
+        to_pair.copy(many, many, {"batch": 1 - c}, 1).wait_send()
+
+
+def finish(*refs):
+    sources, results, sems = refs[:4], refs[4:8], refs[8]
+    copies = [
+        pltpu.make_async_copy(src, dst, sems.at[i])
+        for i, (src, dst) in enumerate(zip(sources, results))
+    ]
+    for copy in copies:
+        copy.start()
+    for copy in copies:
+        copy.wait()
+
+
+GROUPS = 3 + 6 + 4 * 3 + 1 + 1 + 4 + 4 + 1 + 4
 SENT = (
-    3 * 64 + 6 * 256 + 18 * 80 + 28 * 256 + 4 * 320 + 3 * 320
-    + 12 * 96 + 12 * 64 + 15 * 24 + 15 * 16
+    3 * 64 + 6 * 256 + 18 * 80 + 26 * 256 + 4 * 320 + 3 * 320
+    + 12 * 96 + 12 * 64 + 3 * 96 + 3 * 64 + 3 * 40
 )
 
 
 def body(inputs, cotangent, w_query, w_key, w_value):
     vmem = pltpu.VMEM
     hbm = pl.BlockSpec(memory_space=pl.ANY)
-    here = pl.BlockSpec(memory_space=pltpu.VMEM)
     scan = [
         vmem((4, 80, 128), f32), vmem((4, 80, 128), f32), vmem((80, 128), f32),
         vmem((3, 80, 128), f32), vmem((4, 80, 128), f32), vmem((4, 80, 128), f32),
@@ -548,21 +553,22 @@
         vmem((2, 128, TOK), f32), vmem((2, FP, 128), bf16), vmem((2, 8, FP), f32),
         *scan, *scan,
         vmem((2, 4, 320, 128), f32), vmem((4, 320, 128), f32), vmem((BLK, D), bf16),
-        vmem((BLK, D), f32), vmem((4, 4, 96, 128), f32), vmem((4, 4, 64, 128), f32),
-        vmem((4, 3, 96, 128), f32), vmem((3, 4, 64, 128), f32),
-        vmem((4, 4, 24, 128), f32), vmem((16, 24, 128), f32), vmem((16, 16, 128), f32),
-        vmem((4, 40, 128), f32), vmem((SENT, 128), f32),
-        pltpu.SemaphoreType.DMA((8,)), pltpu.SemaphoreType.DMA, pltpu.SemaphoreType.DMA, pltpu.SemaphoreType.DMA,
+        vmem((D, BLK), f32), vmem((4, 4, 96, 128), f32), vmem((4, 4, 64, 128), f32),
+        vmem((4, 3, 96, 128), f32), vmem((2, 4, 64, 128), f32),
+        vmem((4, 96, 128), f32), vmem((3, 96, 128), f32), vmem((3, 64, 128), f32),
+        vmem((4, 64, 128), f32),
+        vmem((4, 40, 128), f32), vmem((4, 40, 128), f32),
+        vmem((4, 40, 128), f32), vmem((16, 128), f32), vmem((16, 128), f32),
+        vmem((16, 1024), f32), vmem((SENT, 128), f32),
+        pltpu.SemaphoreType.DMA((8,)), pltpu.SemaphoreType.DMA((4,)), pltpu.SemaphoreType.DMA((2,)),
         pltpu.SemaphoreType.DMA((GROUPS,)),
     ]
-    gin, res = pl.pallas_call(
+    shapes = (((1, BLK, D), bf16), ((16, 128), f32), ((16, 128), f32), ((16, 1024), f32))
+    results = pl.pallas_call(
         kernel,
-        out_shape=(
-            pltpu.VMEM((1, BLK, D), bf16),
-            pltpu.VMEM((4, 40, 128), f32),
-        ),
+        out_shape=tuple(pltpu.VMEM(*shape) for shape in shapes),
         in_specs=[pl.BlockSpec(memory_space=pltpu.HBM)] * 5,
-        out_specs=(hbm, hbm),
+        out_specs=(hbm,) * 4,
         scratch_shapes=scratch,
         compiler_params=pltpu.CompilerParams(
             collective_id=0, has_side_effects=True, vmem_limit_bytes=60 * 1024 * 1024
@@ -570,17 +576,12 @@
     )(inputs, cotangent, w_query, w_key, w_value)
     return pl.pallas_call(
         finish,
-        out_shape=(
-            jax.ShapeDtypeStruct((1, BLK, D), bf16),
-            jax.ShapeDtypeStruct((16, 128), f32),
-            jax.ShapeDtypeStruct((16, 128), f32),
-            jax.ShapeDtypeStruct((16, 1024), f32),
-        ),
-        in_specs=[hbm] * 2,
-        out_specs=(pl.BlockSpec(memory_space=pltpu.HBM), here, here, here),
-        scratch_shapes=[pltpu.VMEM((4, 40, 128), f32), pltpu.SemaphoreType.DMA((2,))],
+        out_shape=tuple(jax.ShapeDtypeStruct(*shape) for shape in shapes),
+        in_specs=[hbm] * 4,
+        out_specs=(pl.BlockSpec(memory_space=pltpu.HBM),) * 4,
+        scratch_shapes=[pltpu.SemaphoreType.DMA((4,))],
         compiler_params=pltpu.CompilerParams(vmem_limit_bytes=4 * 1024 * 1024),
-    )(gin, res)
+    )(*results)
 
 
 def solution(mesh):

time: 70.2 us -> 69.1 us (0.984)
  the two profiles are of different devices: /device:TPU:0 before, /device:TPU:1 now
where the time goes in v4:
time: 69.1 us; the launch traced here: 69 us
  Pallas kernels  68.3 us (99%)
    pallas_call x1, Pallas kernels, body(): pl.pallas_call(kernel, out_shape=tuple((pltpu.VMEM(*shape) for shape in s...  67.5 us

profile of v4, /device:TPU:1, one launch (start us, length us, event | category | flops | bytes accessed | tf_op | source)
XLA Modules:
  0.0 69.0 jit_solution(12521052954156810027)
XLA Ops:
  0.6 67.5 %shard_map.84 = (bf16[1,128,2048]{2,1,0:T(8,128)(2,1)S(1)}, f32[16,128]{1,0:T(8,128)S(1)}, f32[16,128]{1,0:T(8,128)S(1)}, f32[16,1024]{1,0:T(8,128)S(1)}) custom-call(bf16[1,128,2048]{2,1,0:T(8,128)(2,1)} %x_hbm.1, bf16[1,128,1024]{2,1,0:T(8,128)(2,1)} %u_hbm.1, bf16[2048,128]{1,0:T(8,128)(2,1)} %wq_hbm.1, bf16[2048,128]{1,0:T(8,128)(2,1)} %wk_hbm.1, ...), custom_call_target="tpu_custom_call" | custom-call | tf_op jit(solution)/shard_map/pallas_call | solution.py:567
  68.1 0.8 %shard_map.85 = (bf16[1,128,2048]{2,1,0:T(8,128)(2,1)}, f32[16,128]{1,0:T(8,128)}, f32[16,128]{1,0:T(8,128)}, f32[16,1024]{1,0:T(8,128)}) custom-call(bf16[1,128,2048]{2,1,0:T(8,128)(2,1)S(1)} %get-tuple-element.8.refs_0_, f32[16,128]{1,0:T(8,128)S(1)} %get-tuple-element.9.refs_1_, f32[16,128]{1,0:T(8,128)S(1)} %get-tuple-element.10.refs_2_, ...), custom_call_target="tpu_custom_call" | custom-call | tf_op jit(solution)/shard_map/pallas_call | solution.py:577

commit v5 on v4

--- a/solution.py
+++ b/solution.py
@@ -367,6 +367,7 @@
     x_pass(1)
     local_backward(1)
     move = scan_back(move, xr2, zr2, pb2, pf2, True)
+    x_pass(2)
     for h in range(2):
         lo = 16 * h
         uq = jnp.concatenate([rqk[slot(y, j), lo : lo + 16] for j in range(N)], 1) * 0.5
@@ -388,10 +389,8 @@
         put_grad(h, 288, uk, g_fk)
 
     pair_g = one(gg.at[c], gg.at[c], {"batch": 1 - c})
-    x_pass(2)
     gb[3] = gg[c, y]
     gacc[...] = mm(wv[3], gb[3, 0:256].astype(bf16))
-    x_pass(3)
     pair_g.wait()
     rhs = jnp.concatenate([gg[i, j].astype(bf16) for j in range(N) for i in range(2)], 1)
 
@@ -431,6 +430,7 @@
 
     x_in[0].wait()
     weights_of(0)
+    x_pass(3)
     x_in[1].wait()
     weights_of(1)
     x_in[2].wait()

time: 69.1 us -> 68.7 us (level)
  the two profiles are of different devices: /device:TPU:1 before, /device:TPU:0 now
where the time goes in v5:
time: 68.7 us; the launch traced here: 67.4 us
  Pallas kernels  66.8 us (97%)
    pallas_call x1, Pallas kernels, body(): pl.pallas_call(kernel, out_shape=tuple((pltpu.VMEM(*shape) for shape in s...  65.9 us

profile of v5, /device:TPU:0, one launch (start us, length us, event | category | flops | bytes accessed | tf_op | source)
XLA Modules:
  0.0 67.4 jit_solution(11007469079081108564)
XLA Ops:
  0.6 65.9 %shard_map.84 = (bf16[1,128,2048]{2,1,0:T(8,128)(2,1)S(1)}, f32[16,128]{1,0:T(8,128)S(1)}, f32[16,128]{1,0:T(8,128)S(1)}, f32[16,1024]{1,0:T(8,128)S(1)}) custom-call(bf16[1,128,2048]{2,1,0:T(8,128)(2,1)} %x_hbm.1, bf16[1,128,1024]{2,1,0:T(8,128)(2,1)} %u_hbm.1, bf16[2048,128]{1,0:T(8,128)(2,1)} %wq_hbm.1, bf16[2048,128]{1,0:T(8,128)(2,1)} %wk_hbm.1, ...), custom_call_target="tpu_custom_call" | custom-call | tf_op jit(solution)/shard_map/pallas_call | solution.py:567
  66.6 0.8 %shard_map.85 = (bf16[1,128,2048]{2,1,0:T(8,128)(2,1)}, f32[16,128]{1,0:T(8,128)}, f32[16,128]{1,0:T(8,128)}, f32[16,1024]{1,0:T(8,128)}) custom-call(bf16[1,128,2048]{2,1,0:T(8,128)(2,1)S(1)} %get-tuple-element.8.refs_0_, f32[16,128]{1,0:T(8,128)S(1)} %get-tuple-element.9.refs_1_, f32[16,128]{1,0:T(8,128)S(1)} %get-tuple-element.10.refs_2_, ...), custom_call_target="tpu_custom_call" | custom-call | tf_op jit(solution)/shard_map/pallas_call | solution.py:577

commit v6 on v5

--- a/solution.py
+++ b/solution.py
@@ -84,8 +84,8 @@
     fq, fk, vb, vt, ut, at, num, dloc, gnb, gdr, gfq, gfk, gvt, stb, nrm,
     st1, xr1, zs1, zr1, pb1, pf1,
     st2, xr2, zs2, zr2, pb2, pf2,
-    gg, gb, gi, gacc, da, db, ra, rb, sa, fa, fb, fc, yb, yr, rs, rs_q, rs_k, rs_v, total,
-    lsem, osem, ssem, rsem,
+    gg, gb, gacc, da, db, ra, rb, sa, fa, fb, fc, yb, yr, rs, total,
+    lsem, ssem, rsem,
 ):
     z, x, y, c = (lax.axis_index(a) for a in SEQ_BATCH)
     place = {"seq_0": z, "seq_1": x, "seq_2": y}
@@ -389,8 +389,6 @@
         put_grad(h, 288, uk, g_fk)
 
     pair_g = one(gg.at[c], gg.at[c], {"batch": 1 - c})
-    gb[3] = gg[c, y]
-    gacc[...] = mm(wv[3], gb[3, 0:256].astype(bf16))
     pair_g.wait()
     rhs = jnp.concatenate([gg[i, j].astype(bf16) for j in range(N) for i in range(2)], 1)
 
@@ -437,6 +435,8 @@
     weights_of(2)
     g_thin = Group(gb.at[pl.ds(0, 3), pl.ds(256, 64)])
     a_onward(0)
+    gb[3] = gg[c, y]
+    gacc[...] = mm(wv[3], gb[3, 0:256].astype(bf16))
     x_in[3].wait()
     g_wide = {}
     for dy in (2, 1, 3):
@@ -480,9 +480,7 @@
     part = jnp.concatenate([gb[2, 0:256], gb[0, 0:256]], 0).astype(bf16)
     gacc[...] = gacc[...] + mm(jnp.concatenate([wv[0], wv[1]], 1), part)
     for i in range(16):
-        gi[:, 128 * i : 128 * i + 128] = gacc[128 * i : 128 * i + 128].T.astype(bf16)
-    out_copy = pltpu.make_async_copy(gi, gin.at[0], osem.at[0])
-    out_copy.start()
+        gin[0, :, 128 * i : 128 * i + 128] = gacc[128 * i : 128 * i + 128].T.astype(bf16)
     y_in.wait()
     for dy in range(N):
         rs[at_peer("seq_2", (4 - dy) % 4)] = yr[(dy + 3) % 4]
@@ -490,22 +488,16 @@
     w_q = jnp.zeros((16, 128), f32)
     w_k = jnp.zeros((16, 128), f32)
     for p in range(N):
-        rs_v[:, 256 * p : 256 * p + 128] = rs[p, 0:16]
-        rs_v[:, 256 * p + 128 : 256 * p + 256] = rs[p, 24:40]
+        gwv[:, 256 * p : 256 * p + 128] = rs[p, 0:16]
+        gwv[:, 256 * p + 128 : 256 * p + 256] = rs[p, 24:40]
         thin = rs[p, 16:24]
         thin = jnp.concatenate([thin, pltpu.roll(thin, 64, 1)], 0)
         from_q = pltpu.roll(thin, 32 * p, 1) if p else thin
         w_q = jnp.where(lane == p, from_q, w_q)
         from_k = pltpu.roll(thin, (32 * p + 96) % 128, 1) if p != 1 else thin
         w_k = jnp.where(lane == p, from_k, w_k)
-    rs_q[...] = w_q
-    rs_k[...] = w_k
-    results = [out_copy]
-    for i, (src, dst) in enumerate(((rs_q, gwq), (rs_k, gwk), (rs_v, gwv))):
-        results.append(pltpu.make_async_copy(src, dst, osem.at[i + 1]))
-        results[-1].start()
-    for copy in results:
-        copy.wait()
+    gwq[...] = w_q
+    gwk[...] = w_k
     assert groups[0] == GROUPS and bytes_sent[0] == SENT * 512
     to_pair.copy(total, total, {"batch": 1 - c}).wait_send()
 
@@ -552,15 +544,14 @@
         vmem((2, 8, TOK), f32), vmem((2, FP, TOK), f32), vmem((2, FP, TOK), f32),
         vmem((2, 128, TOK), f32), vmem((2, FP, 128), bf16), vmem((2, 8, FP), f32),
         *scan, *scan,
-        vmem((2, 4, 320, 128), f32), vmem((4, 320, 128), f32), vmem((BLK, D), bf16),
+        vmem((2, 4, 320, 128), f32), vmem((4, 320, 128), f32),
         vmem((D, BLK), f32), vmem((4, 4, 96, 128), f32), vmem((4, 4, 64, 128), f32),
         vmem((4, 3, 96, 128), f32), vmem((2, 4, 64, 128), f32),
         vmem((4, 96, 128), f32), vmem((3, 96, 128), f32), vmem((3, 64, 128), f32),
         vmem((4, 64, 128), f32),
         vmem((4, 40, 128), f32), vmem((4, 40, 128), f32),
-        vmem((4, 40, 128), f32), vmem((16, 128), f32), vmem((16, 128), f32),
-        vmem((16, 1024), f32), vmem((SENT, 128), f32),
-        pltpu.SemaphoreType.DMA((8,)), pltpu.SemaphoreType.DMA((4,)), pltpu.SemaphoreType.DMA((2,)),
+        vmem((4, 40, 128), f32), vmem((SENT, 128), f32),
+        pltpu.SemaphoreType.DMA((8,)), pltpu.SemaphoreType.DMA((2,)),
         pltpu.SemaphoreType.DMA((GROUPS,)),
     ]
     shapes = (((1, BLK, D), bf16), ((16, 128), f32), ((16, 128), f32), ((16, 1024), f32))
@@ -568,7 +559,7 @@
         kernel,
         out_shape=tuple(pltpu.VMEM(*shape) for shape in shapes),
         in_specs=[pl.BlockSpec(memory_space=pltpu.HBM)] * 5,
-        out_specs=(hbm,) * 4,
+        out_specs=(pl.BlockSpec(memory_space=pltpu.VMEM),) * 4,
         scratch_shapes=scratch,
         compiler_params=pltpu.CompilerParams(
             collective_id=0, has_side_effects=True, vmem_limit_bytes=60 * 1024 * 1024

time: 68.7 us -> 68.6 us (level)
  no operation moved by 1% of the time
where the time goes in v6:
time: 68.6 us; the launch traced here: 67.3 us
  Pallas kernels  66.6 us (97%)
    pallas_call x1, Pallas kernels, body(): pl.pallas_call(kernel, out_shape=tuple((pltpu.VMEM(*shape) for shape in s...  65.8 us

profile of v6, /device:TPU:0, one launch (start us, length us, event | category | flops | bytes accessed | tf_op | source)
XLA Modules:
  0.0 67.3 jit_solution(1887377946994527213)
XLA Ops:
  0.6 65.8 %shard_map.84 = (bf16[1,128,2048]{2,1,0:T(8,128)(2,1)S(1)}, f32[16,128]{1,0:T(8,128)S(1)}, f32[16,128]{1,0:T(8,128)S(1)}, f32[16,1024]{1,0:T(8,128)S(1)}) custom-call(bf16[1,128,2048]{2,1,0:T(8,128)(2,1)} %x_hbm.1, bf16[1,128,1024]{2,1,0:T(8,128)(2,1)} %u_hbm.1, bf16[2048,128]{1,0:T(8,128)(2,1)} %wq_hbm.1, bf16[2048,128]{1,0:T(8,128)(2,1)} %wk_hbm.1, ...), custom_call_target="tpu_custom_call" | custom-call | tf_op jit(solution)/shard_map/pallas_call | solution.py:558
  66.4 0.8 %shard_map.85 = (bf16[1,128,2048]{2,1,0:T(8,128)(2,1)}, f32[16,128]{1,0:T(8,128)}, f32[16,128]{1,0:T(8,128)}, f32[16,1024]{1,0:T(8,128)}) custom-call(bf16[1,128,2048]{2,1,0:T(8,128)(2,1)S(1)} %get-tuple-element.8.refs_0_, f32[16,128]{1,0:T(8,128)S(1)} %get-tuple-element.9.refs_1_, f32[16,128]{1,0:T(8,128)S(1)} %get-tuple-element.10.refs_2_, ...), custom_call_target="tpu_custom_call" | custom-call | tf_op jit(solution)/shard_map/pallas_call | solution.py:568

commit v7 on v6

--- a/solution.py
+++ b/solution.py
@@ -389,6 +389,8 @@
         put_grad(h, 288, uk, g_fk)
 
     pair_g = one(gg.at[c], gg.at[c], {"batch": 1 - c})
+    gb[3] = gg[c, y]
+    gacc[...] = mm(wv[3], gb[3, 0:256].astype(bf16))
     pair_g.wait()
     rhs = jnp.concatenate([gg[i, j].astype(bf16) for j in range(N) for i in range(2)], 1)
 
@@ -435,8 +437,6 @@
     weights_of(2)
     g_thin = Group(gb.at[pl.ds(0, 3), pl.ds(256, 64)])
     a_onward(0)
-    gb[3] = gg[c, y]
-    gacc[...] = mm(wv[3], gb[3, 0:256].astype(bf16))
     x_in[3].wait()
     g_wide = {}
     for dy in (2, 1, 3):
@@ -446,13 +446,13 @@
         p = at_peer("seq_2", dy)
         g_wide[dy] = one(gg.at[c, p, pl.ds(0, 256)], gb.at[dy - 1, pl.ds(0, 256)], {"seq_2": p})
     weights_of(3)
+    a_onward(1)
     b_in.wait()
     for xx in range(N):
         db[3, xx] = db[3, xx] + (rb[0, xx] + rb[1, xx])
     for d in (1, 3, 2):
         p = at_peer("seq_1", d)
         b_last.send(db.at[3, p], fb.at[d - 1], {"seq_1": p})
-    a_onward(1)
     a_onward(2)
 
     a_onward(3)

time: 68.6 us -> 68.6 us (level)
  no operation moved by 1% of the time
where the time goes in v7:
time: 68.6 us; the launch traced here: 67.3 us
  Pallas kernels  66.6 us (97%)
    pallas_call x1, Pallas kernels, body(): pl.pallas_call(kernel, out_shape=tuple((pltpu.VMEM(*shape) for shape in s...  65.8 us

profile of v7, /device:TPU:0, one launch (start us, length us, event | category | flops | bytes accessed | tf_op | source)
XLA Modules:
  0.0 67.3 jit_solution(17998443064205287975)
XLA Ops:
  0.6 65.8 %shard_map.84 = (bf16[1,128,2048]{2,1,0:T(8,128)(2,1)S(1)}, f32[16,128]{1,0:T(8,128)S(1)}, f32[16,128]{1,0:T(8,128)S(1)}, f32[16,1024]{1,0:T(8,128)S(1)}) custom-call(bf16[1,128,2048]{2,1,0:T(8,128)(2,1)} %x_hbm.1, bf16[1,128,1024]{2,1,0:T(8,128)(2,1)} %u_hbm.1, bf16[2048,128]{1,0:T(8,128)(2,1)} %wq_hbm.1, bf16[2048,128]{1,0:T(8,128)(2,1)} %wk_hbm.1, ...), custom_call_target="tpu_custom_call" | custom-call | tf_op jit(solution)/shard_map/pallas_call | solution.py:558
  66.4 0.8 %shard_map.85 = (bf16[1,128,2048]{2,1,0:T(8,128)(2,1)}, f32[16,128]{1,0:T(8,128)}, f32[16,128]{1,0:T(8,128)}, f32[16,1024]{1,0:T(8,128)}) custom-call(bf16[1,128,2048]{2,1,0:T(8,128)(2,1)S(1)} %get-tuple-element.8.refs_0_, f32[16,128]{1,0:T(8,128)S(1)} %get-tuple-element.9.refs_1_, f32[16,128]{1,0:T(8,128)S(1)} %get-tuple-element.10.refs_2_, ...), custom_call_target="tpu_custom_call" | custom-call | tf_op jit(solution)/shard_map/pallas_call | solution.py:568
